TPU v7x, 16 devices: a 4x2x1 block of a 4x4x8 slice. The times are simulated.
16 devices in a mesh: rep: 2 (over y, z), dp: 8 (over x, core).
Axes of the slice: x: 4, y: 2, z: 1, core: 2. Of those that a mesh axis runs over, the one named last changes fastest.
The devices are a block of a 4x4x8 slice.
Arguments:
- x: bfloat16 [16, 2048, 896], P(('rep', 'dp')), parts along dimension 0
- dy: bfloat16 [16, 2048, 896], P(('rep', 'dp')), parts along dimension 0
- w_gate: bfloat16 [2, 896, 2560], replicated
- w_up: bfloat16 [2, 896, 2560], replicated
- w_down: bfloat16 [2, 2560, 896], replicated
- m_w_gate: float32 [2, 896, 2560], P(None, 'dp')
- m_w_up: float32 [2, 896, 2560], P(None, 'dp')
- m_w_down: float32 [2, 2560, 896], P(None, 'dp')
- v_w_gate: float32 [2, 896, 2560], P(None, 'dp')
- v_w_up: float32 [2, 896, 2560], P(None, 'dp')
- v_w_down: float32 [2, 2560, 896], P(None, 'dp')
Outputs:
- output 1: bfloat16 [4, 896, 2560], P('rep'), parts along dimension 0
- output 2: bfloat16 [4, 896, 2560], P('rep'), parts along dimension 0
- output 3: bfloat16 [4, 2560, 896], P('rep'), parts along dimension 0
- output 4: float32 [4, 896, 2560], P('rep', 'dp'), parts along dimension 0
- output 5: float32 [4, 896, 2560], P('rep', 'dp'), parts along dimension 0
- output 6: float32 [4, 2560, 896], P('rep', 'dp'), parts along dimension 0
- output 7: float32 [4, 896, 2560], P('rep', 'dp'), parts along dimension 0
- output 8: float32 [4, 896, 2560], P('rep', 'dp'), parts along dimension 0
- output 9: float32 [4, 2560, 896], P('rep', 'dp'), parts along dimension 0
There are 2 independent parts. A program takes and returns all parts, laid end to end along the dimension named above; an argument that names none is the same for every part.
All inputs are finite; a program needn't handle non-finite values.
Results may differ from a plain program's by a relative error of at most 0.022.
Values are sent between devices in bfloat16 or wider.
A program may use at most 768 MiB of HBM per device.

v0:
```python
import jax
import jax.numpy as jnp
from jax import lax

NAMES = ("w_gate", "w_up", "w_down")


def matmul(a, w):
    return jnp.dot(a, w, preferred_element_type=jnp.float32).astype(jnp.bfloat16)


def normed(h):
    wide = h.astype(jnp.float32)
    scale = lax.rsqrt(jnp.mean(wide**2, -1, keepdims=True) + 1e-6)
    return (wide * scale).astype(jnp.bfloat16)


def layer(h, w):
    a = normed(h)
    gate = jnp.dot(a, w["w_gate"], preferred_element_type=jnp.float32)
    up = jnp.dot(a, w["w_up"], preferred_element_type=jnp.float32)
    return h + matmul((jax.nn.silu(gate) * up).astype(jnp.bfloat16), w["w_down"])


def adamw(w, m, v, g):
    m = 0.9 * m + 0.1 * g
    v = 0.95 * v + 0.05 * g * g
    step = m * lax.rsqrt(v + 1e-8) + 0.1 * w
    return (w - 0.02 * step).astype(jnp.bfloat16), m, v


def clipped(gradients, sum_of_squares, count):
    factor = jnp.minimum(1.0, 0.5 * lax.rsqrt(sum_of_squares / count + 1e-30))
    return [g * factor for g in gradients]


def stack(weights, h):
    for number in range(weights["w_gate"].shape[0]):
        h = layer(h, {name: w[number] for name, w in weights.items()})
    return h


def solution(mesh):
    groups = mesh.shape["rep"]

    def step(x, dy, *arrays):
        weights, m, v = (arrays[i : i + 3] for i in (0, 3, 6))
        x, dy = (t.reshape(groups, -1, *t.shape[1:]) for t in (x, dy))

        def of_a_group(x, dy):
            _, back = jax.vjp(lambda w: stack(w, x), dict(zip(NAMES, weights, strict=True)))
            by_weights = back(dy)[0]
            gradients = [by_weights[name].astype(jnp.float32) for name in NAMES]
            gradients = clipped(gradients, sum(jnp.sum(g * g) for g in gradients), sum(g.size for g in gradients))
            new = [adamw(w.astype(jnp.float32), m, v, g) for w, m, v, g in zip(weights, m, v, gradients, strict=True)]
            return tuple(one[which] for which in range(3) for one in new)

        return tuple(t.reshape(-1, *t.shape[2:]) for t in jax.vmap(of_a_group)(x, dy))

    return step
```

profile of v0, /device:TPU:113, one launch (start us, length us, event | category | flops | bytes accessed | tf_op | source)
XLA Modules:
  0.0 756.9 jit_solution(7394765137304199456)
XLA Ops:
  16.1 14.2 %fusion.67 = f32[2048,2560]{1,0:T(8,128)S(1)} fusion(bf16[2,896,2560]{2,1,0:T(8,128)(2,1)} %param, bf16[1,2048,896]{2,1,0:T(8,128)(2,1)} %param.2, f32[2048]{0:T(1024)S(1)} %add_rsqrt_fusion), kind=kOutput, calls=%fused_computation.79 | convolution fusion | flops 9400745984 | bytes 29237248 | tf_op jit(solution)/vmap(jvp())/dot_general | solution.py:20
  30.4 22.5 %fusion.65 = f32[2048,2560]{1,0:T(8,128)} fusion(bf16[2,896,2560]{2,1,0:T(8,128)(2,1)} %param.3, bf16[1,2048,896]{2,1,0:T(8,128)(2,1)} %param.2, f32[2048]{0:T(1024)S(1)} %add_rsqrt_fusion), kind=kOutput, calls=%fused_computation.77 | convolution fusion | flops 9400745984 | bytes 29237248 | tf_op jit(solution)/vmap(jvp())/dot_general | solution.py:21
  52.8 15.2 %fusion.26 = bf16[2048,2560]{1,0:T(8,128)(2,1)} fusion(f32[2048,2560]{1,0:T(8,128)} %fusion.65, f32[2048,2560]{1,0:T(8,128)S(1)} %fusion.67), kind=kLoop, calls=%fused_computation.41 | loop fusion | flops 31457280 | bytes 52428800
  68.1 15.4 %fusion.39 = (f32[2048]{0:T(1024)S(1)}, bf16[1,1,2048,896]{2,3,1,0:T(8,128)(2,1)S(1)}) fusion(bf16[2048,2560]{1,0:T(8,128)(2,1)} %fusion.26, bf16[2,2560,896]{2,1,0:T(8,128)(2,1)} %param.4, bf16[1,2048,896]{1,2,0:T(8,128)(2,1)} %copy), kind=kOutput, calls=%fused_computation.56 | convolution fusion | flops 9404413952 | bytes 22421504 | tf_op jit(solution)/vmap(jvp())/dot_general | solution.py:9
  83.5 18.5 %fusion.54 = f32[2048,2560]{1,0:T(8,128)} fusion(bf16[2,896,2560]{2,1,0:T(8,128)(2,1)} %param, bf16[1,1,2048,896]{2,3,1,0:T(8,128)(2,1)S(1)} %get-tuple-element.10, f32[2048]{0:T(1024)S(1)} %bitcast.351), kind=kOutput, calls=%fused_computation.66 | convolution fusion | flops 9400745984 | bytes 29237248 | tf_op jit(solution)/vmap(jvp())/dot_general | solution.py:20
  102.0 17.4 %fusion.58 = f32[2048,2560]{1,0:T(8,128)} fusion(bf16[2,896,2560]{2,1,0:T(8,128)(2,1)} %param.3, bf16[1,1,2048,896]{2,3,1,0:T(8,128)(2,1)S(1)} %get-tuple-element.10, f32[2048]{0:T(1024)S(1)} %bitcast.352), kind=kOutput, calls=%fused_computation.70 | convolution fusion | flops 9400745984 | bytes 29237248 | tf_op jit(solution)/vmap(jvp())/dot_general | solution.py:21
  119.4 15.6 %convolution_convert_fusion.1 = bf16[2048,2560]{1,0:T(8,128)(2,1)} fusion(bf16[2,2560,896]{2,1,0:T(8,128)(2,1)} %param.4, bf16[1,2048,896]{2,1,0:T(8,128)(2,1)S(1)} %copy-done.2), kind=kOutput, calls=%fused_computation.40 | convolution fusion | flops 9400483840 | bytes 18743296 | tf_op jit(solution)/vmap(transpose(jvp()))/dot_general | solution.py:9
  141.1 22.5 %fusion.6 = bf16[2048,2560]{1,0:T(8,128)(2,1)} fusion(f32[2048,2560]{1,0:T(8,128)} %fusion.54, f32[2048,2560]{1,0:T(8,128)} %fusion.58, bf16[2048,2560]{1,0:T(8,128)(2,1)} %convolution_convert_fusion.1), kind=kLoop, calls=%fused_computation.11 | loop fusion | flops 62914560 | bytes 62914560
  163.6 15.3 %fusion.56 = bf16[2048,896]{0,1:T(8,128)(2,1)} fusion(bf16[2048,2560]{1,0:T(8,128)(2,1)} %fusion.6, bf16[2,896,2560]{2,1,0:T(8,128)(2,1)} %param), kind=kOutput, calls=%fused_computation.68 | convolution fusion | flops 9395240960 | bytes 18743296 | tf_op jit(solution)/vmap(transpose(jvp()))/dot_general | solution.py:20
  178.9 20.5 %fusion.41 = (f32[2048]{0:T(1024)}, bf16[2048,896]{0,1:T(8,128)(2,1)}) fusion(bf16[1,1,2048,896]{2,3,1,0:T(8,128)(2,1)S(1)} %copy-done.4, bf16[2048,896]{0,1:T(8,128)(2,1)} %fusion.56, bf16[2,896,2560]{2,1,0:T(8,128)(2,1)} %param.3, bf16[2048,2560]{1,0:T(8,128)(2,1)} %convolution_convert_fusion.1, f32[2048,2560]{1,0:T(8,128)} %fusion.54), kind=kOutput, calls=%fused_computation.58 | convolution fusion | flops 9437706240 | bytes 47063040 | tf_op jit(solution)/vmap(transpose(jvp()))/dot_general | solution.py:21
  206.8 15.8 %convolution_bitcast_fusion = f32[1,2560,896]{2,1,0:T(8,128)} fusion(bf16[2048,2560]{1,0:T(8,128)(2,1)S(1)} %bitcast.344, bf16[2048,896]{0,1:T(8,128)(2,1)} %fusion.81), kind=kOutput, calls=%fused_computation.64 | convolution fusion | flops 9395240960 | bytes 23330816 | tf_op jit(solution)/vmap(transpose(jvp()))/dot_general | solution.py:9
  222.7 21.9 %fusion.42 = f32[1,2560,896]{2,1,0:T(8,128)} fusion(f32[2048,2560]{1,0:T(8,128)} %fusion.58, f32[2048,2560]{1,0:T(8,128)} %fusion.54, bf16[1,2048,896]{2,1,0:T(8,128)(2,1)} %param.5), kind=kOutput, calls=%fused_computation.60 | convolution fusion | flops 9426698240 | bytes 54788096 | tf_op jit(solution)/vmap(transpose(jvp()))/dot_general | solution.py:9
  244.8 16.7 %convolution_convert_fusion = bf16[2048,2560]{1,0:T(8,128)(2,1)} fusion(bf16[2048,896]{0,1:T(8,128)(2,1)} %fusion.81, bf16[2,2560,896]{2,1,0:T(8,128)(2,1)} %param.4), kind=kOutput, calls=%fused_computation.39 | convolution fusion | flops 9400483840 | bytes 18743296 | tf_op jit(solution)/vmap(transpose(jvp()))/dot_general | solution.py:9
  261.5 19.2 %fusion.51 = f32[1,896,2560]{2,1,0:T(8,128)} fusion(bf16[2048,2560]{1,0:T(8,128)(2,1)} %convolution_convert_fusion, f32[2048,2560]{1,0:T(8,128)} %copy-done, bf16[1,2048,896]{1,2,0:T(8,128)(2,1)} %copy, f32[2048]{0:T(1024)S(1)} %copy-done.8), kind=kOutput, calls=%fused_computation.63 | convolution fusion | flops 9432203264 | bytes 44310528 | tf_op jit(solution)/vmap(transpose(jvp()))/dot_general | solution.py:21
  281.4 19.5 %fusion.45 = f32[1,896,2560]{2,1,0:T(8,128)} fusion(bf16[2048,2560]{1,0:T(8,128)(2,1)} %convolution_convert_fusion.1, f32[2048,2560]{1,0:T(8,128)} %fusion.54, bf16[1,1,2048,896]{2,3,1,0:T(8,128)(2,1)} %copy-done.3, f32[2048]{0:T(1024)S(1)} %bitcast.354), kind=kOutput, calls=%fused_computation.61 | convolution fusion | flops 9432203264 | bytes 44310528 | tf_op jit(solution)/vmap(transpose(jvp()))/dot_general | solution.py:21
  301.0 26.4 %fusion.48 = f32[1,896,2560]{2,1,0:T(8,128)} fusion(f32[2048,2560]{1,0:T(8,128)} %copy-done, f32[2048,2560]{1,0:T(8,128)} %fusion.65, bf16[2048,2560]{1,0:T(8,128)(2,1)} %convolution_convert_fusion, bf16[1,2048,896]{1,2,0:T(8,128)(2,1)} %copy, f32[2048]{0:T(1024)S(1)} %copy-done.8), kind=kOutput, calls=%fused_computation.62 | convolution fusion | flops 9458417664 | bytes 65282048 | tf_op jit(solution)/vmap(transpose(jvp()))/dot_general | solution.py:20
  327.5 15.8 %convolution_bitcast_fusion.1 = f32[1,896,2560]{2,1,0:T(8,128)} fusion(bf16[2048,2560]{1,0:T(8,128)(2,1)} %fusion.6, bf16[1,1,2048,896]{2,3,1,0:T(8,128)(2,1)} %copy-done.3, f32[2048]{0:T(1024)S(1)} %bitcast.355), kind=kOutput, calls=%fused_computation.65 | convolution fusion | flops 9400745984 | bytes 23339008 | tf_op jit(solution)/vmap(transpose(jvp()))/dot_general | solution.py:20
  349.1 37.2 %reduce-scatter.25.cloned.1.call-done = f32[1,112,2560]{2,1,0:T(8,128)} async-done(((f32[1,896,2560]{2,1,0:T(8,128)}), f32[1,112,2560]{2,1,0:T(8,128)}) %reduce-scatter.25.cloned.1.call-update) | async-done | bytes 1146896
  387.6 52.7 %reduce-scatter.23.cloned.1.call-done = f32[1,112,2560]{2,1,0:T(8,128)} async-done(((f32[1,896,2560]{2,1,0:T(8,128)}), f32[1,112,2560]{2,1,0:T(8,128)}) %reduce-scatter.23.cloned.1.call-update) | async-done | bytes 1146896
  442.8 52.1 %reduce-scatter.21.cloned.1.call-done = f32[1,112,2560]{2,1,0:T(8,128)} async-done(((f32[1,896,2560]{2,1,0:T(8,128)}), f32[1,112,2560]{2,1,0:T(8,128)}) %reduce-scatter.21.cloned.1.call-update) | async-done | bytes 1146896
  496.2 53.3 %reduce-scatter.19.cloned.1.call-done = f32[1,112,2560]{2,1,0:T(8,128)} async-done(((f32[1,896,2560]{2,1,0:T(8,128)}), f32[1,112,2560]{2,1,0:T(8,128)}) %reduce-scatter.19.cloned.1.call-update) | async-done | bytes 1146896
  588.4 35.4 %all-gather.14.cloned.1.call-done = bf16[1,2,2560,896]{3,2,1,0:T(8,128)(2,1)} async-done(((bf16[1,2,320,896]{3,2,1,0:T(8,128)(2,1)}), bf16[1,2,2560,896]{3,2,1,0:T(8,128)(2,1)}) %all-gather.14.cloned.1.call-update) | async-done | bytes 9175056 | tf_op jit(solution)/reshape | solution.py:58
  623.8 51.2 %all-gather.12.cloned.1.call-done = bf16[1,2,896,2560]{3,2,1,0:T(8,128)(2,1)} async-done(((bf16[1,2,112,2560]{3,2,1,0:T(8,128)(2,1)}), bf16[1,2,896,2560]{3,2,1,0:T(8,128)(2,1)}) %all-gather.12.cloned.1.call-update) | async-done | bytes 9175056 | tf_op jit(solution)/reshape | solution.py:58
  675.0 51.2 %all-gather.10.cloned.1.call-done = bf16[1,2,896,2560]{3,2,1,0:T(8,128)(2,1)} async-done(((bf16[1,2,112,2560]{3,2,1,0:T(8,128)(2,1)}), bf16[1,2,896,2560]{3,2,1,0:T(8,128)(2,1)}) %all-gather.10.cloned.1.call-update) | async-done | bytes 9175056 | tf_op jit(solution)/reshape | solution.py:58
  (72 shorter events, 93.6 us)
Async XLA Ops:
  7.2 338.1 %reduce-scatter.29.cloned.1.call-start = ((), (), s32[]{:S(2)}) async-start(), calls=%async_computation.14 | async-start | bytes 10321920
  16.1 14.2 %copy-start.7 = (f32[2048]{0:T(1024)}, f32[2048]{0:T(1024)S(1)}, u32[]{:S(2)}) copy-start(f32[2048]{0:T(1024)S(1)} %add_rsqrt_fusion) | copy-start | bytes 24580
  30.4 22.5 %copy-start = (f32[2048,2560]{1,0:T(8,128)}, f32[2048,2560]{1,0:T(8,128)S(1)}, u32[]{:S(2)}) copy-start(f32[2048,2560]{1,0:T(8,128)S(1)} %fusion.67) | copy-start | bytes 62914564
  83.5 18.5 %copy-start.3 = (bf16[1,1,2048,896]{2,3,1,0:T(8,128)(2,1)}, bf16[1,1,2048,896]{2,3,1,0:T(8,128)(2,1)S(1)}, u32[]{:S(2)}) copy-start(bf16[1,1,2048,896]{2,3,1,0:T(8,128)(2,1)S(1)} %get-tuple-element.10) | copy-start | bytes 11010052
  83.5 18.5 %copy-start.5 = (f32[1,1,2048]{2,1,0:T(1,128)}, f32[1,1,2048]{2,1,0:T(1,128)S(1)}, u32[]{:S(2)}) copy-start(f32[1,1,2048]{2,1,0:T(1,128)S(1)} %rsqrt.38) | copy-start | bytes 24580
  102.0 17.4 %copy-start.2 = (bf16[1,2048,896]{2,1,0:T(8,128)(2,1)S(1)}, bf16[1,2048,896]{2,1,0:T(8,128)(2,1)}, u32[]{:S(2)}) copy-start(bf16[1,2048,896]{2,1,0:T(8,128)(2,1)} %param.5) | copy-start | bytes 11010052
  163.6 15.3 %copy-start.4 = (bf16[1,1,2048,896]{2,3,1,0:T(8,128)(2,1)S(1)}, bf16[1,1,2048,896]{2,3,1,0:T(8,128)(2,1)}, u32[]{:S(2)}) copy-start(bf16[1,1,2048,896]{2,3,1,0:T(8,128)(2,1)} %copy-done.3) | copy-start | bytes 11010052
  163.6 43.2 %slice-start = ((s8[10485760]{0:T(1024)(128)(4,1)}), s8[4194304]{0:T(1024)(128)(4,1)S(1)}, s32[]{:S(2)}) async-start(s8[10485760]{0:T(1024)(128)(4,1)} %bitcast.343), calls=%async_computation.15 | async-start | bytes 8388608
  178.9 21.3 %copy-start.1 = (bf16[1,2048,896]{1,2,0:T(8,128)(2,1)S(1)}, bf16[1,2048,896]{1,2,0:T(8,128)(2,1)}, u32[]{:S(2)}) copy-start(bf16[1,2048,896]{1,2,0:T(8,128)(2,1)} %copy.1) | copy-start | bytes 11010052
  178.9 27.8 %slice-start.1 = ((s8[10485760]{0:T(1024)(128)(4,1)}), s8[4194304]{0:T(1024)(128)(4,1)S(1)}, s32[]{:S(2)}) async-start(s8[10485760]{0:T(1024)(128)(4,1)} %bitcast.343), calls=%async_computation.16 | async-start | bytes 8388608
  178.9 27.8 %slice-start.2 = ((s8[10485760]{0:T(1024)(128)(4,1)}), s8[2097152]{0:T(1024)(128)(4,1)S(1)}, s32[]{:S(2)}) async-start(s8[10485760]{0:T(1024)(128)(4,1)} %bitcast.343), calls=%async_computation.17 | async-start | bytes 4194304
  222.6 124.0 %reduce-scatter.27.cloned.1.call-start = ((), (), s32[]{:S(2)}) async-start(), calls=%async_computation.13 | async-start | bytes 10321920
  244.7 16.8 %copy-start.8 = (f32[2048]{0:T(1024)S(1)}, f32[2048]{0:T(1024)}, u32[]{:S(2)}) copy-start(f32[2048]{0:T(1024)} %copy-done.7) | copy-start | bytes 24580
  244.7 141.6 %reduce-scatter.25.cloned.1.call-start = ((), (), s32[]{:S(2)}) async-start(), calls=%async_computation.12 | async-start | bytes 10321920
  280.7 0.7 copy-start.6
  280.8 159.6 %reduce-scatter.23.cloned.1.call-start = ((), (), s32[]{:S(2)}) async-start(), calls=%async_computation.11 | async-start | bytes 10321920
  300.9 194.0 %reduce-scatter.21.cloned.1.call-start = ((), (), s32[]{:S(2)}) async-start(), calls=%async_computation.10 | async-start | bytes 10321920
  327.4 222.1 %reduce-scatter.19.cloned.1.call-start = ((), (), s32[]{:S(2)}) async-start(), calls=%async_computation.9 | async-start | bytes 10321920
  343.3 0.7 copy-start.9
  343.4 280.4 %all-gather.14.cloned.1.call-start = ((), (), s32[]{:S(2)}) async-start(), calls=%async_computation.8 | async-start | bytes 10321920 | tf_op jit(solution)/reshape | solution.py:58
  575.3 99.7 %all-gather.12.cloned.1.call-start = ((), (), s32[]{:S(2)}) async-start(), calls=%async_computation.7 | async-start | bytes 10321920 | tf_op jit(solution)/reshape | solution.py:58
  581.9 144.4 %all-gather.10.cloned.1.call-start = ((), (), s32[]{:S(2)}) async-start(), calls=%async_computation.6 | async-start | bytes 10321920 | tf_op jit(solution)/reshape | solution.py:58
Sparse Core Ops, SparseCore 0:
  222.7 54.5 reduce-scatter.28
  279.7 51.8 reduce-scatter.26
  334.4 51.8 reduce-scatter.24
  388.5 51.8 reduce-scatter.22
  443.1 51.8 reduce-scatter.20
  497.7 51.8 reduce-scatter.18
  575.4 48.3 all-gather.13
  626.0 49.0 all-gather.11
  677.2 49.0 all-gather.9
where the time goes:
time: 766 us; the launch traced here: 757 us
  waiting for transfers between devices  334 us (44%)
  matrix products  275 us (36%)
  other arithmetic  78.7 us (10%)
  local copies, waits for them, and re-layouts  37.5 us (5%)
  between operations  17.8 us (2%)
  blocking collectives  14 us (2%)
    unnamed x15, waiting for transfers between devices  196 us
    reshape x3, waiting for transfers between devices, step(): t.reshape(-1, *t.shape[2:])  138 us
    dot_general x5, matrix products, layer(): up = jnp.dot(a, w['w_up'], preferred_element_type=jnp.float32)  99 us
    dot_general x5, matrix products, layer(): gate = jnp.dot(a, w['w_gate'], preferred_element_type=jnp.float32)  90.2 us
    dot_general x5, matrix products, matmul(): jnp.dot(a, w, preferred_element_type=jnp.float32).astype(jnp.bfloat16)  85.5 us
    unnamed x4, other arithmetic  44.3 us
    unnamed x31, local copies, waits for them, and re-layouts  36.9 us
    reshape x3, other arithmetic, step(): t.reshape(-1, *t.shape[2:])  19.4 us
  transfers between devices with their start and end apart: 9, of which 7 were waited for; matrix products, arithmetic and copies ran while one was open for 19% of the time, Pallas kernels for 0%

commit v1 on v0

v1 whole, which is shorter than its diff:
```python
import functools

import jax
import jax.numpy as jnp
from jax import lax
from jax.experimental import pallas as pl
from jax.experimental.pallas import tpu as pltpu
from jax.sharding import PartitionSpec as P

F32, BF16 = jnp.float32, jnp.bfloat16
VMEM_LIMIT = 63 * 1024 * 1024
NT = (((1,), (1,)), ((), ()))
TILE = 512
ROWS = 256


def dot(a, b, dims=(((1,), (0,)), ((), ()))):
    return lax.dot_general(a, b, dims, preferred_element_type=F32)


def scale_of(wide):
    return lax.rsqrt(jnp.mean(wide * wide, -1, keepdims=True) + 1e-6)


def normed(h):
    wide = h.astype(F32)
    return (wide * scale_of(wide)).astype(BF16)


def chunks(total, size):
    return [slice(at, min(at + size, total)) for at in range(0, total, size)]


def gated(gate, up, dact):
    s = jax.nn.sigmoid(gate)
    silu = gate * s
    return (dact * up * (s + silu * (1 - s))).astype(BF16), (dact * silu).astype(BF16)


def rows_kernel(x, dy, wg0, wu0, wd0, wg1, wu1, wd1, b, at, gate0, up0):
    cols = chunks(wg0.shape[1], 512)
    a = normed(x[...])
    at[3] = a.T
    for c in cols:
        gate, up = dot(a, wg0[:, c]), dot(a, wu0[:, c])
        gate0[:, c], up0[:, c] = gate, up
        b[3, :, c] = (jax.nn.silu(gate) * up).astype(BF16)
    h = x[...] + dot(b[3], wd0[...]).astype(BF16)
    a = normed(h)
    at[1] = a.T
    d = dy[...]
    at[0] = d.T
    for c in cols:
        gate, up = dot(a, wg1[:, c]), dot(a, wu1[:, c])
        dact = dot(d, wd1[c, :], NT).astype(BF16).astype(F32)
        b[0, :, c] = (jax.nn.silu(gate) * up).astype(BF16)
        b[1, :, c], b[2, :, c] = gated(gate, up, dact)
    da = dot(b[1], wg1[...], NT).astype(BF16) + dot(b[2], wu1[...], NT).astype(BF16)
    da, wide = da.astype(F32), h.astype(F32)
    scale = scale_of(wide)
    inner = jnp.mean(da * wide, -1, keepdims=True)
    d = d + (da * scale - wide * (scale * scale * scale * inner)).astype(BF16)
    at[2] = d.T
    for c in cols:
        dact = dot(d, wd0[c, :], NT).astype(BF16).astype(F32)
        b[4, :, c], b[5, :, c] = gated(gate0[:, c], up0[:, c], dact)


def row_local(x, dy, wg, wu, wd):
    t, d = x.shape
    f = wg.shape[2]
    resident = lambda w, n: pl.BlockSpec((pl.squeezed, *w.shape[1:]), lambda i: (n, 0, 0), pipeline_mode=pl.Buffered(1))
    rows = pl.BlockSpec((ROWS, d), lambda i: (i, 0))
    return pl.pallas_call(
        rows_kernel,
        grid=(t // ROWS,),
        in_specs=[rows, rows] + [resident(w, n) for n in (0, 1) for w in (wg, wu, wd)],
        out_specs=[pl.BlockSpec((6, ROWS, f), lambda i: (0, i, 0)), pl.BlockSpec((4, d, ROWS), lambda i: (0, 0, i))],
        out_shape=[jax.ShapeDtypeStruct((6, t, f), BF16), jax.ShapeDtypeStruct((4, d, t), BF16)],
        scratch_shapes=[pltpu.VMEM((ROWS, f), F32), pltpu.VMEM((ROWS, f), F32)],
        compiler_params=pltpu.CompilerParams(vmem_limit_bytes=VMEM_LIMIT),
        cost_estimate=pl.CostEstimate(flops=18 * t * d * f, bytes_accessed=150 * 2**20, transcendentals=0),
        name="rows",
    )(x, dy, wg, wu, wd, wg, wu, wd)


class Place:
    def __init__(self, devices):
        assert devices == 8
        self.devices = devices
        self.me = lax.axis_index("dp")
        self.chip, self.core = self.me // 2, self.me % 2

    def block(self, step):
        return (self.chip + step) % 4 * 2 + self.core

    def sibling_block(self, step):
        return (self.chip + step) % 4 * 2 + 1 - self.core

    def barrier(self, peers):
        semaphore = pltpu.get_barrier_semaphore()
        for peer in peers:
            pl.semaphore_signal(semaphore, inc=1, device_id={"dp": peer}, device_id_type=pl.DeviceIdType.MESH)
        pl.semaphore_wait(semaphore, len(peers))


def send(src, dst, sems, at, to):
    return pltpu.make_async_remote_copy(
        src_ref=src, dst_ref=dst, send_sem=sems[0].at[at], recv_sem=sems[1].at[at], device_id={"dp": to}, device_id_type=pl.DeviceIdType.MESH
    )


def each_row(count, body, size=16):
    lax.fori_loop(0, count // size, lambda i, c: body(pl.ds(pl.multiple_of(i * size, size), size), c) or c, 0)


def grads_kernel(
    devices, at, b, out_wide, out_tall, out_total, wide, tall, sib_wide, sib_tall, transit_wide, transit_tall, end_wide, end_tall, part, totals, sends, recvs
):
    step = pl.program_id(0)
    per = b.shape[1] and wide.shape[2] // TILE
    which, tile = step // per, step % per
    place = Place(devices)
    me = place.me
    peers = [(me + j) % devices for j in range(1, devices)]
    sibling = place.sibling_block(0)
    sems = (sends, recvs)
    low, high = wide.shape[1] // devices, tall.shape[0] // devices

    @pl.when(step == 0)
    def _():
        part[...] = jnp.zeros_like(part)
        place.barrier(peers)

    class Sum:
        def __init__(self, k):
            self.k, self.is_tall = k, k % 3 == 0
            n = k // 3
            if self.is_tall:
                self.rows, self.mine, self.sib = high, tall, sib_tall
                self.transit, self.end, self.out = [transit_tall.at[n, i] for i in (0, 1)], [end_tall.at[n, i] for i in (0, 1)], out_tall.at[n]
                self.halves = [(pl.ds(i * high // 2, high // 2), slice(None)) for i in (0, 1)]
            else:
                slot = k % 3 - 1
                self.rows, self.mine, self.sib = low, wide.at[slot], sib_wide.at[slot]
                at = 2 * n + slot
                self.transit, self.end, self.out = [transit_wide.at[at, i] for i in (0, 1)], [end_wide.at[at, i] for i in (0, 1)], out_wide.at[at]
                c = wide.shape[2] // 2
                self.halves = [(slice(None), slice(i * c, (i + 1) * c)) for i in (0, 1)]

        def block(self, number):
            return self.mine.at[pl.ds(pl.multiple_of(number * self.rows, 16), self.rows), :]

        def half(self, number, i):
            rows, cols = self.halves[i]
            start, size = (i * self.rows // 2, self.rows // 2) if self.is_tall else (0, self.rows)
            return self.mine.at[pl.ds(pl.multiple_of(number * self.rows + start, 16), size), cols]

        def to_sibling(self, j):
            return send(self.block(place.sibling_block(j)), self.sib.at[j], sems, (self.k, j), sibling)

        def in_transit(self, i):
            return send(self.half(place.block(2), i), self.transit[i], sems, (self.k, 4 + i), place.block(1 - 2 * i))

        def to_end(self, i, j):
            return send(self.half(place.block(1 - 2 * i), j), self.end[i].at[self.halves[j]], sems, (self.k, (8 if i == j else 6) + i), place.block(1 - 2 * i))

        def start(self):
            for j in (2, 1, 3, 0):
                self.to_sibling(j).start()

        def first(self):
            for j in (2, 1, 3, 0):
                self.to_sibling(j).wait_recv()
                mine, theirs = self.block(place.block(j)), self.sib.at[j]

                def add(rows, _):
                    mine[rows, :] = (mine[rows, :].astype(F32) + theirs[rows, :].astype(F32)).astype(BF16)

                each_row(self.rows, add)
                if j == 2:
                    for i in (0, 1):
                        self.in_transit(i).start()
                if j in (1, 3):
                    i = j // 2
                    self.to_end(i, 1 - i).start()

        def second(self):
            for i in (0, 1):
                self.in_transit(i).wait_recv()
                mine, theirs = self.half(place.block(1 - 2 * i), i), self.transit[i]

                def add(rows, _):
                    mine[rows, :] = (mine[rows, :].astype(F32) + theirs[rows, :].astype(F32)).astype(BF16)

                each_row(mine.shape[0], add)
                self.to_end(i, i).start()

        def last(self):
            for i in (0, 1):
                for j in (0, 1):
                    self.to_end(i, j).wait_recv()
            mine = self.block(me)

            def add(rows, total):
                g = (mine[rows, :].astype(F32) + self.end[0][rows, :].astype(F32) + self.end[1][rows, :].astype(F32)).astype(BF16)
                self.out[rows, :] = g
                g = g.astype(F32)
                return total + g[:8] * g[:8] + g[8:] * g[8:]

            cols = mine.shape[1]
            square = lax.fori_loop(0, self.rows // 16, lambda i, c: add(pl.ds(pl.multiple_of(i * 16, 16), 16), c), jnp.zeros((8, cols), F32))
            for c in chunks(cols, 128):
                part[...] += square[:, c]
            for j in (2, 1, 3, 0):
                self.to_sibling(j).wait_send()
            for i in (0, 1):
                self.in_transit(i).wait_send()
                for j in (0, 1):
                    self.to_end(i, j).wait_send()

    sums = [Sum(k) for k in range(6)]
    for k in range(4):
        pl.when(step == per * (k + 2) + 2)(sums[k].last)
    for k in range(5):
        pl.when(step == per * (k + 1) + 2)(sums[k].first)
        pl.when(step == per * (k + 2) - 1)(sums[k].second)

    @pl.when(which % 3 == 0)
    def _():
        tall[pl.ds(pl.multiple_of(tile * TILE, TILE), TILE), :] = dot(at[...], b[...]).T.astype(BF16)

    @pl.when(which % 3 != 0)
    def _():
        wide[which % 3 - 1, :, pl.ds(pl.multiple_of(tile * TILE, TILE), TILE)] = dot(at[...], b[...]).astype(BF16)

    for k in range(6):
        pl.when(step == per * (k + 1) - 1)(sums[k].start)

    @pl.when(step == per * 6 - 1)
    def _():
        sums[5].first()
        sums[4].last()
        sums[5].second()
        sums[5].last()
        exchange = [send(part, totals.at[j], sems, (6, j), peer) for j, peer in enumerate(peers)]
        for copy in exchange:
            copy.start()
        total = part[...]
        for copy in exchange:
            copy.wait_recv()
        for j in range(len(peers)):
            total += totals[j]
        out_total[...] = total
        for copy in exchange:
            copy.wait_send()


def summed_gradients(at, b, devices):
    (_, d, t), f = at.shape, b.shape[2]
    low, high, per = d // devices, f // devices, f // TILE
    vmem = pltpu.VMEM
    whole = lambda *shape: pl.BlockSpec(shape, lambda i: (0,) * len(shape))
    operand = lambda i: ((i // per % 3 + 1) // 2 + 2 * (i // per // 3), 0, 0)
    return pl.pallas_call(
        functools.partial(grads_kernel, devices),
        grid=(6 * per,),
        in_specs=[pl.BlockSpec((pl.squeezed, d, t), operand), pl.BlockSpec((pl.squeezed, t, TILE), lambda i: (i // per, 0, i % per))],
        out_specs=[whole(4, low, f), whole(2, high, d), whole(8, 128)],
        out_shape=[jax.ShapeDtypeStruct((4, low, f), BF16), jax.ShapeDtypeStruct((2, high, d), BF16), jax.ShapeDtypeStruct((8, 128), F32)],
        scratch_shapes=[
            vmem((2, d, f), BF16), vmem((f, d), BF16), vmem((2, 4, low, f), BF16), vmem((4, high, d), BF16),
            vmem((4, 2, low, f // 2), BF16), vmem((2, 2, high // 2, d), BF16), vmem((4, 2, low, f), BF16), vmem((2, 2, high, d), BF16),
            vmem((8, 128), F32), vmem((devices - 1, 8, 128), F32),
            pltpu.SemaphoreType.DMA((7, 10)), pltpu.SemaphoreType.DMA((7, 10)),
        ],
        compiler_params=pltpu.CompilerParams(vmem_limit_bytes=VMEM_LIMIT, collective_id=0, has_side_effects=True),
        cost_estimate=pl.CostEstimate(flops=12 * t * d * f, bytes_accessed=80 * 2**20, transcendentals=0),
        name="grads",
    )(at, b)


def gather_kernel(devices, *refs):
    count = (len(refs) - 3) // 2
    own, full, (local, sends, recvs) = refs[:count], refs[count : 2 * count], refs[2 * count :]
    place = Place(devices)
    me, right, left, sibling = place.me, place.block(1), place.block(3), place.sibling_block(0)
    place.barrier([right, left, sibling])
    pieces = [(a, n) for n in (0, 1) for a in range(count)]

    class Piece:
        def __init__(self, k):
            self.k = k
            self.a, self.n = pieces[k]
            self.rows = own[self.a].shape[1]
            self.by_rows = own[self.a].shape[1] > 128
            self.mine = own[self.a].at[self.n]

        def at(self, number):
            return full[self.a].at[self.n, pl.ds(pl.multiple_of(number * self.rows, 16), self.rows), :]

        def half(self, number, i):
            if self.by_rows:
                size = self.rows // 2
                return full[self.a].at[self.n, pl.ds(pl.multiple_of(number * self.rows + i * size, 16), size), :]
            size = full[self.a].shape[2] // 2
            return full[self.a].at[self.n, pl.ds(pl.multiple_of(number * self.rows, 16), self.rows), pl.ds(i * size, size)]

        def to(self, i):
            return send(self.mine, self.at(me), (sends, recvs), (self.k, i), (right, left, sibling)[i])

        def came(self, i):
            block = self.at((left, right, sibling)[i])
            return send(block, block, (sends, recvs), (self.k, i), sibling)

        def on(self, i):
            block = self.half((left, right)[i], i)
            return send(block, block, (sends, recvs), (self.k, 3 + i), (right, left)[i])

        def opposite(self, i):
            block = self.half(place.block(2), i)
            return send(block, block, (sends, recvs), (self.k, 3 + i), sibling)

        def across(self, i):
            block = self.at((left, right)[i]) if i < 2 else self.half(place.block(2), i - 2)
            return send(block, block, (sends, recvs), (self.k, 5 + i), sibling)

        def came_across(self, i):
            step = (3, 1, 2, 2)[i]
            block = self.at(place.sibling_block(step)) if i < 2 else self.half(place.sibling_block(2), i - 2)
            return send(block, block, (sends, recvs), (self.k, 5 + i), sibling)

        def keep(self):
            return pltpu.make_async_copy(self.mine, self.at(me), local.at[self.k])

        def start(self):
            for i in range(3):
                self.to(i).start()
            self.keep().start()

        def relay(self):
            for i in (0, 1):
                self.came(i).wait_recv()
                self.on(i).start()
                self.across(i).start()

        def finish(self):
            for i in (0, 1):
                self.opposite(i).wait_recv()
                self.across(2 + i).start()

        def end(self):
            self.keep().wait()
            self.came(2).wait_recv()
            for i in range(3):
                self.to(i).wait_send()
            for i in (0, 1):
                self.on(i).wait_send()
            for i in range(4):
                self.across(i).wait_send()
                self.came_across(i).wait_recv()

    work = [Piece(k) for k in range(len(pieces))]
    for k in range(2):
        work[k].start()
    for k in range(len(work)):
        work[k].relay()
        if k + 2 < len(work):
            work[k + 2].start()
        if k:
            work[k - 1].finish()
    work[-1].finish()
    for piece in work:
        piece.end()


def gathered(own, devices):
    return pl.pallas_call(
        functools.partial(gather_kernel, devices),
        in_specs=[pl.BlockSpec(memory_space=pltpu.VMEM)] * len(own),
        out_specs=[pl.BlockSpec(memory_space=pl.ANY)] * len(own),
        out_shape=[jax.ShapeDtypeStruct((w.shape[0], devices * w.shape[1], w.shape[2]), w.dtype) for w in own],
        scratch_shapes=[pltpu.SemaphoreType.DMA((6,)), pltpu.SemaphoreType.DMA((6, 9)), pltpu.SemaphoreType.DMA((6, 9))],
        compiler_params=pltpu.CompilerParams(vmem_limit_bytes=VMEM_LIMIT, collective_id=1, has_side_effects=True),
        name="gather",
    )(*own)


def adamw(w, m, v, g):
    m = 0.9 * m + 0.1 * g
    v = 0.95 * v + 0.05 * g * g
    step = m * lax.rsqrt(v + 1e-8) + 0.1 * w
    return (w - 0.02 * step).astype(BF16), m, v


def solution(mesh):
    devices = mesh.shape["dp"]

    def body(x, dy, wg, wu, wd, *moments):
        ms, vs = moments[:3], moments[3:]
        b, at = row_local(x[0], dy[0], wg, wu, wd)
        wide, tall, total = summed_gradients(at, b, devices)
        grads = [jnp.stack([wide[2], wide[0]]), jnp.stack([wide[3], wide[1]]), jnp.stack([tall[1], tall[0]])]
        factor = jnp.minimum(1.0, 0.5 * lax.rsqrt(jnp.sum(total) / sum(w.size for w in (wg, wu, wd)) + 1e-30))
        me = lax.axis_index("dp")
        new = []
        for w, m, v, g in zip((wg, wu, wd), ms, vs, grads, strict=True):
            own = lax.dynamic_slice_in_dim(w, me * m.shape[1], m.shape[1], 1).astype(F32)
            new.append(adamw(own, m, v, g.astype(F32) * factor))
        new_w, new_m, new_v = zip(*new, strict=True)
        return (*gathered(new_w, devices), *new_m, *new_v)

    data, whole, rows = P(("rep", "dp")), P(), P(None, "dp")
    return jax.shard_map(
        body,
        mesh=mesh,
        in_specs=(data, data, whole, whole, whole, *[rows] * 6),
        out_specs=(*[P("rep")] * 3, *[P("rep", "dp")] * 6),
        check_vma=False,
    )
```

time: 766 us -> 439 us (0.57); the launches traced: 757 us -> 439 us
  Pallas kernels: 0 us -> 396 us
  waiting for transfers between devices: 334 us -> 0 us
  matrix products: 275 us -> 0 us
  other arithmetic: 78.7 us -> 12.8 us
  between operations: 17.8 us -> 1.4 us
  blocking collectives: 14 us -> 0 us
  local copies, waits for them, and re-layouts: 37.5 us -> 28.7 us
    pallas_call x0 -> x3, Pallas kernels: none -> 396 us  [the longest x1 152 us: summed_gradients(): pl.pallas_call(functools.partial(grads_kernel, devices), grid=(6 * per,),...]
    dot_general x15 -> x0, matrix products: 275 us -> none  [the longest x5 99 us: layer(): up = jnp.dot(a, w['w_up'], preferred_element_type=jnp.float32)]
    unnamed x15 -> x0, waiting for transfers between devices: 196 us -> none
    reshape x3 -> x0, waiting for transfers between devices: 138 us -> none  [step(): t.reshape(-1, *t.shape[2:])]
    unnamed x4 -> x0, other arithmetic: 44.3 us -> none
    reshape x3 -> x0, other arithmetic: 19.4 us -> none  [step(): t.reshape(-1, *t.shape[2:])]
    reduce_sum x1 -> x0, blocking collectives: 14 us -> none  [of_a_group(): jnp.sum(g * g)]
    convert_element_type x0 -> x2, other arithmetic: none -> 11.6 us  [adamw(): return ((w - 0.02 * step).astype(BF16), m, v)]
  transfers between devices with their start and end apart: 9 -> 0, of which waited for: 7 -> 0; matrix products, arithmetic and copies ran while one was open for 19% -> 0% of each run, Pallas kernels for 0% -> 0%
where the time goes in v1:
time: 439 us
  Pallas kernels  396 us (90%)
  local copies, waits for them, and re-layouts  28.7 us (7%)
  other arithmetic  12.8 us (3%)
    pallas_call x1, Pallas kernels, summed_gradients(): pl.pallas_call(functools.partial(grads_kernel, devices), grid=(6 * per,),...  152 us
    pallas_call x1, Pallas kernels, row_local(): pl.pallas_call(rows_kernel, grid=(t // ROWS,), in_specs=[rows, rows] + [r...  125 us
    pallas_call x1, Pallas kernels, gathered(): pl.pallas_call(functools.partial(gather_kernel, devices), in_specs=[pl.Bl...  119 us
    unnamed x17, local copies, waits for them, and re-layouts  26.7 us
    convert_element_type x2, other arithmetic, adamw(): return ((w - 0.02 * step).astype(BF16), m, v)  11.6 us

profile of v1, /device:TPU:113, one launch (start us, length us, event | category | flops | bytes accessed | tf_op | source)
XLA Modules:
  0.0 438.9 jit_solution(13429476932985418830)
XLA Ops:
  0.6 125.1 %rows.1 = (bf16[6,2048,2560]{2,1,0:T(8,128)(2,1)}, bf16[4,896,2048]{2,1,0:T(8,128)(2,1)}) custom-call(bf16[2048,896]{1,0:T(8,128)(2,1)} %bitcast.2, bf16[2048,896]{1,0:T(8,128)(2,1)} %bitcast.3, bf16[2,896,2560]{2,1,0:T(8,128)(2,1)} %wg1.1, bf16[2,896,2560]{2,1,0:T(8,128)(2,1)} %wu1.1, bf16[2,2560,896]{2,1,0:T(8,128)(2,1)} %wd1.1, ...), custom_call_target="tpu_custom_call" | custom-call | flops 84557168640 | bytes 157286400 | tf_op jit(solution)/shard_map/rows/pallas_call | solution.py:74
  125.7 151.7 %grads.1 = (bf16[4,112,2560]{2,1,0:T(8,128)(2,1)}, bf16[2,320,896]{2,1,0:T(8,128)(2,1)}, f32[8,128]{1,0:T(8,128)}) custom-call(bf16[4,896,2048]{2,1,0:T(8,128)(2,1)} %get-tuple-element.17.at, bf16[6,2048,2560]{2,1,0:T(8,128)(2,1)} %get-tuple-element.18.b), custom_call_target="tpu_custom_call" | custom-call | flops 56371445760 | bytes 83886080 | tf_op jit(solution)/shard_map/grads/pallas_call | solution.py:265
  277.4 1.3 reduce_sum.9
  279.4 0.0 copy-start.6
  279.4 0.0 copy-start.1
  279.4 1.9 fusion.15
  281.3 0.0 copy-start
  281.3 0.0 copy-done.6
  281.3 0.1 fusion.16
  281.4 0.6 copy-done.1
  282.1 1.0 copy-done
  283.1 0.0 copy-start.2
  283.1 0.0 copy-start.3
  283.1 0.0 copy-start.4
  283.1 4.8 %fusion.8 = (bf16[2,320,896]{2,1,0:T(8,128)(2,1)}, f32[2,320,896]{2,1,0:T(8,128)}, f32[2,320,896]{2,1,0:T(8,128)}) fusion(bf16[2,2560,896]{2,1,0:T(8,128)(2,1)} %wd1.1, s32[]{:T(128)S(6)} %select_n.8, f32[]{:T(128)S(6)} %min_shard_map.3, bf16[1,320,896]{2,1,0:T(8,128)(2,1)S(1)} %get-tuple-element.39, bf16[1,320,896]{2,1,0:T(8,128)(2,1)S(1)} %get-tuple-element.38, ...), kind=kLoop, calls=%fused_computation.17 | loop fusion | flops 11468800 | bytes 12615688 | tf_op jit(solution)/shard_map/convert_element_type | solution.py:393
  287.9 0.0 copy-done.2
  287.9 0.0 copy-done.3
  287.9 0.0 copy-done.4
  287.9 1.3 copy-done.5
  289.2 6.8 %fusion.2 = (bf16[2,112,2560]{2,1,0:T(8,128)(2,1)}, f32[2,112,2560]{2,1,0:T(8,128)}, f32[2,112,2560]{2,1,0:T(8,128)}, bf16[2,112,2560]{2,1,0:T(8,128)(2,1)}, f32...) fusion(bf16[2,896,2560]{2,1,0:T(8,128)(2,1)} %wg1.1, s32[]{:T(128)S(6)} %select_n.7, f32[]{:T(128)S(6)} %min_shard_map.3, ...), kind=kLoop, calls=%fused_computation.11 | loop fusion | flops 22937600 | bytes 25231368 | tf_op jit(solution)/shard_map/convert_element_type | solution.py:393
  295.9 119.3 %gather.1 = (bf16[2,896,2560]{2,1,0:T(8,128)(2,1)}, bf16[2,896,2560]{2,1,0:T(8,128)(2,1)}, bf16[2,2560,896]{2,1,0:T(8,128)(2,1)}) custom-call(bf16[2,112,2560]{2,1,0:T(8,128)(2,1)} %get-tuple-element.31.refs_0_, bf16[2,112,2560]{2,1,0:T(8,128)(2,1)} %get-tuple-element.40.refs_1_, bf16[2,320,896]{2,1,0:T(8,128)(2,1)} %get-tuple-element.25.refs_2_), custom_call_target="tpu_custom_call" | custom-call | tf_op jit(solution)/shard_map/gather/pallas_call | solution.py:378
  415.2 7.9 %copy.23 = bf16[2,896,2560]{2,1,0:T(8,128)(2,1)} copy(bf16[2,896,2560]{2,1,0:T(8,128)(2,1)} %get-tuple-element.52) | data formatting | bytes 18350080
  423.1 7.8 %copy.24 = bf16[2,896,2560]{2,1,0:T(8,128)(2,1)} copy(bf16[2,896,2560]{2,1,0:T(8,128)(2,1)} %get-tuple-element.53) | data formatting | bytes 18350080
  430.9 8.0 %copy.25 = bf16[2,2560,896]{2,1,0:T(8,128)(2,1)} copy(bf16[2,2560,896]{2,1,0:T(8,128)(2,1)} %get-tuple-element.54) | data formatting | bytes 18350080
  (1 shorter events, 0.0 us)
Async XLA Ops:
  279.4 1.9 copy-start.6
  279.4 2.7 copy-start.1
  281.3 1.8 copy-start
  283.1 4.8 %copy-start.2 = (f32[2,112,2560]{2,1,0:T(8,128)S(1)}, f32[2,112,2560]{2,1,0:T(8,128)}, u32[]{:S(2)}) copy-start(f32[2,112,2560]{2,1,0:T(8,128)} %param.19) | copy-start | bytes 6881284
  283.1 4.8 %copy-start.3 = (f32[2,112,2560]{2,1,0:T(8,128)S(1)}, f32[2,112,2560]{2,1,0:T(8,128)}, u32[]{:S(2)}) copy-start(f32[2,112,2560]{2,1,0:T(8,128)} %param.16) | copy-start | bytes 6881284
  283.1 4.8 %copy-start.4 = (f32[2,112,2560]{2,1,0:T(8,128)S(1)}, f32[2,112,2560]{2,1,0:T(8,128)}, u32[]{:S(2)}) copy-start(f32[2,112,2560]{2,1,0:T(8,128)} %param.20) | copy-start | bytes 6881284
  283.1 6.1 %copy-start.5 = (f32[2,112,2560]{2,1,0:T(8,128)S(1)}, f32[2,112,2560]{2,1,0:T(8,128)}, u32[]{:S(2)}) copy-start(f32[2,112,2560]{2,1,0:T(8,128)} %param.17) | copy-start | bytes 6881284

commit v2 on v1

v2 whole, which is shorter than its diff:
```python
import functools

import jax
import jax.numpy as jnp
from jax import lax
from jax.experimental import pallas as pl
from jax.experimental.pallas import tpu as pltpu
from jax.sharding import PartitionSpec as P

F32, BF16 = jnp.float32, jnp.bfloat16
VMEM_LIMIT = 63 * 1024 * 1024
NT = (((1,), (1,)), ((), ()))
GRADS_LIMIT = 59 * 1024 * 1024
ROWS = 256


def dot(a, b, dims=(((1,), (0,)), ((), ()))):
    return lax.dot_general(a, b, dims, preferred_element_type=F32)


def scale_of(wide):
    return lax.rsqrt(jnp.mean(wide * wide, -1, keepdims=True) + 1e-6)


def normed(h):
    wide = h.astype(F32)
    return (wide * scale_of(wide)).astype(BF16)


def chunks(total, size):
    return [slice(at, min(at + size, total)) for at in range(0, total, size)]


def gated(gate, up, dact):
    s = jax.nn.sigmoid(gate)
    silu = gate * s
    return (dact * up * (s + silu * (1 - s))).astype(BF16), (dact * silu).astype(BF16)


def rows_kernel(x, dy, wg, wu, wd, b, at, gate0, up0, held_wide, held_down, arrived):
    order = [(wg.at[0], held_wide.at[0]), (wu.at[0], held_wide.at[1]), (wd.at[0], held_down.at[0])]
    order += [(wg.at[1], held_wide.at[2]), (wu.at[1], held_wide.at[3]), (wd.at[1], held_down.at[1])]
    copies = [pltpu.make_async_copy(src, dst, arrived.at[n]) for n, (src, dst) in enumerate(order)]
    first = pl.program_id(0) == 0

    @pl.when(first)
    def _():
        for copy in copies:
            copy.start()

    def need(*which):
        @pl.when(first)
        def _():
            for n in which:
                copies[n].wait()

    wg0, wu0, wd0, wg1, wu1, wd1 = (dst for _, dst in order)
    cols = chunks(wg.shape[2], 512)
    a = normed(x[...])
    at[3] = a.T
    d = dy[...]
    at[0] = d.T
    need(0, 1)
    for c in cols:
        gate, up = dot(a, wg0[:, c]), dot(a, wu0[:, c])
        gate0[:, c], up0[:, c] = gate, up
        b[4, :, c] = (jax.nn.silu(gate) * up).astype(BF16)
    need(2)
    h = x[...] + dot(b[4], wd0[...]).astype(BF16)
    a = normed(h)
    at[1] = a.T
    need(3, 4, 5)
    for c in cols:
        gate, up = dot(a, wg1[:, c]), dot(a, wu1[:, c])
        dact = dot(d, wd1[c, :], NT).astype(BF16).astype(F32)
        b[1, :, c] = (jax.nn.silu(gate) * up).astype(BF16)
        b[0, :, c], b[2, :, c] = gated(gate, up, dact)
    da = dot(b[0], wg1[...], NT).astype(BF16) + dot(b[2], wu1[...], NT).astype(BF16)
    da, wide = da.astype(F32), h.astype(F32)
    scale = scale_of(wide)
    inner = jnp.mean(da * wide, -1, keepdims=True)
    d = d + (da * scale - wide * (scale * scale * scale * inner)).astype(BF16)
    at[2] = d.T
    for c in cols:
        dact = dot(d, wd0[c, :], NT).astype(BF16).astype(F32)
        b[3, :, c], b[5, :, c] = gated(gate0[:, c], up0[:, c], dact)


def row_local(x, dy, wg, wu, wd):
    t, d = x.shape
    f = wg.shape[2]
    rows, anywhere = pl.BlockSpec((ROWS, d), lambda i: (i, 0)), pl.BlockSpec(memory_space=pl.ANY)
    return pl.pallas_call(
        rows_kernel,
        grid=(t // ROWS,),
        in_specs=[rows, rows] + [anywhere] * 3,
        out_specs=[pl.BlockSpec((6, ROWS, f), lambda i: (0, i, 0)), pl.BlockSpec((4, d, ROWS), lambda i: (0, 0, i))],
        out_shape=[jax.ShapeDtypeStruct((6, t, f), BF16), jax.ShapeDtypeStruct((4, d, t), BF16)],
        scratch_shapes=[
            pltpu.VMEM((ROWS, f), F32), pltpu.VMEM((ROWS, f), F32), pltpu.VMEM((4, d, f), BF16), pltpu.VMEM((2, f, d), BF16),
            pltpu.SemaphoreType.DMA((6,)),
        ],
        compiler_params=pltpu.CompilerParams(vmem_limit_bytes=VMEM_LIMIT),
        cost_estimate=pl.CostEstimate(flops=18 * t * d * f, bytes_accessed=150 * 2**20, transcendentals=0),
        name="rows",
    )(x, dy, wg, wu, wd)


class Place:
    def __init__(self, devices):
        assert devices == 8
        self.devices = devices
        self.me = lax.axis_index("dp")
        self.chip, self.core = self.me // 2, self.me % 2

    def block(self, step):
        return (self.chip + step) % 4 * 2 + self.core

    def sibling_block(self, step):
        return (self.chip + step) % 4 * 2 + 1 - self.core

    def barrier(self, peers):
        semaphore = pltpu.get_barrier_semaphore()
        for peer in peers:
            pl.semaphore_signal(semaphore, inc=1, device_id={"dp": peer}, device_id_type=pl.DeviceIdType.MESH)
        pl.semaphore_wait(semaphore, len(peers))


def send(src, dst, sems, at, to):
    return pltpu.make_async_remote_copy(
        src_ref=src, dst_ref=dst, send_sem=sems[0].at[at], recv_sem=sems[1].at[at], device_id={"dp": to}, device_id_type=pl.DeviceIdType.MESH
    )


def each_row(count, body, size=16):
    lax.fori_loop(0, count // size, lambda i, c: body(pl.ds(pl.multiple_of(i * size, size), size), c) or c, 0)


def grads_kernel(
    devices, at, b, out_wide, out_tall, out_total, wide, tall, sib_wide, sib_tall, transit_wide, transit_tall, end_wide, end_tall, part, totals, sends, recvs
):
    step = pl.program_id(0)
    which, side = step // 2, step % 2
    place = Place(devices)
    me = place.me
    peers = [(me + j) % devices for j in range(1, devices)]
    sibling = place.sibling_block(0)
    sems = (sends, recvs)
    low, high = wide.shape[1] // devices, tall.shape[0] // devices
    width = wide.shape[2]

    @pl.when(step == 0)
    def _():
        part[...] = jnp.zeros_like(part)
        place.barrier(peers)

    class Sum:
        def __init__(self, number, k, part):
            self.number, n = number, k // 3
            self.is_tall = k % 3 == 1
            self.ready = 4 * (k + 1) - (2 if part == 0 else 0)
            if self.is_tall:
                self.rows, self.cols, self.mine, self.sib = high, slice(None), tall, sib_tall
                self.transit, self.end, self.out = [transit_tall.at[n, i] for i in (0, 1)], [end_tall.at[n, i] for i in (0, 1)], out_tall.at[n]
                self.halves = [(pl.ds(i * high // 2, high // 2), slice(None)) for i in (0, 1)]
            else:
                slot = k % 3 // 2
                at = 2 * n + slot
                start, size = (0, width) if part is None else (part * width // 2, width // 2)
                self.rows, self.cols, self.mine, self.sib = low, pl.ds(start, size), wide.at[slot], sib_wide.at[slot]
                c = size // 2
                self.transit = [transit_wide.at[at, i, :, pl.ds(start // 2, c)] for i in (0, 1)]
                self.end, self.out = [end_wide.at[at, i] for i in (0, 1)], out_wide.at[at]
                self.halves = [(slice(None), pl.ds(start + i * c, c)) for i in (0, 1)]

        def block(self, number):
            return self.mine.at[pl.ds(pl.multiple_of(number * self.rows, 16), self.rows), self.cols]

        def half(self, number, i):
            start, size = (i * self.rows // 2, self.rows // 2) if self.is_tall else (0, self.rows)
            return self.mine.at[pl.ds(pl.multiple_of(number * self.rows + start, 16), size), self.halves[i][1]]

        def theirs(self, j):
            return self.sib.at[j, :, self.cols]

        def to_sibling(self, j):
            return send(self.block(place.sibling_block(j)), self.theirs(j), sems, (self.number, j), sibling)

        def in_transit(self, i):
            return send(self.half(place.block(2), i), self.transit[i], sems, (self.number, 4 + i), place.block(1 - 2 * i))

        def to_end(self, i, j):
            copy = (8 if i == j else 6) + i
            return send(self.half(place.block(1 - 2 * i), j), self.end[i].at[self.halves[j]], sems, (self.number, copy), place.block(1 - 2 * i))

        def start(self):
            for j in (2, 1, 3, 0):
                self.to_sibling(j).start()

        def add(self, mine, theirs):
            def add(rows, _):
                mine[rows, :] = (mine[rows, :].astype(F32) + theirs[rows, :].astype(F32)).astype(BF16)

            each_row(mine.shape[0], add)

        def first(self):
            for j in (2, 1, 3, 0):
                self.to_sibling(j).wait_recv()
                self.add(self.block(place.block(j)), self.theirs(j))
                if j == 2:
                    for i in (0, 1):
                        self.in_transit(i).start()
                if j in (1, 3):
                    self.to_end(j // 2, 1 - j // 2).start()

        def second(self):
            for i in (0, 1):
                self.in_transit(i).wait_recv()
                self.add(self.half(place.block(1 - 2 * i), i), self.transit[i])
                self.to_end(i, i).start()

        def last(self):
            for i in (0, 1):
                for j in (0, 1):
                    self.to_end(i, j).wait_recv()
            mine, out = self.block(me), self.out.at[:, self.cols]
            ends = [end.at[:, self.cols] for end in self.end]

            def add(rows, total):
                g = (mine[rows, :].astype(F32) + ends[0][rows, :].astype(F32) + ends[1][rows, :].astype(F32)).astype(BF16)
                out[rows, :] = g
                g = g.astype(F32)
                return total + g[:8] * g[:8] + g[8:] * g[8:]

            cols = mine.shape[1]
            square = lax.fori_loop(0, self.rows // 16, lambda i, c: add(pl.ds(pl.multiple_of(i * 16, 16), 16), c), jnp.zeros((8, cols), F32))
            for c in chunks(cols, 128):
                part[...] += square[:, c]
            for j in (2, 1, 3, 0):
                self.to_sibling(j).wait_send()
            for i in (0, 1):
                self.in_transit(i).wait_send()
                for j in (0, 1):
                    self.to_end(i, j).wait_send()

    sums = [Sum(n, *of) for n, of in enumerate(((0, 0), (0, 1), (1, None), (2, None), (3, None), (4, None), (5, 0), (5, 1)))]
    moves = []
    for n, one in enumerate(sums):
        after = sums[n + 1].ready + 3 if n + 1 < len(sums) else one.ready + 4
        moves += [(one.ready, 0, one.start), (one.ready + 1, 1, one.first), (one.ready + 3, 2, one.second), (after, 3, one.last)]
    moves.sort(key=lambda move: move[:2])

    def at_point(point):
        for due, _, move in moves:
            if due % 2 == point and due < 24:
                pl.when(step == due // 2)(move)

    def compute(start, size):
        cols = pl.ds(start, size)

        @pl.when(which % 3 == 1)
        def _():
            tall[pl.ds(pl.multiple_of(side * (width // 2) + start, 256), size), :] = dot(at[...], b[:, cols]).astype(BF16).T

        @pl.when(which % 3 != 1)
        def _():
            wide[which % 3 // 2, :, pl.ds(pl.multiple_of(side * (width // 2) + start, 256), size)] = dot(at[...], b[:, cols]).astype(BF16)

    at_point(0)
    compute(0, 512)
    at_point(1)
    compute(512, width // 2 - 512)

    @pl.when(step == 11)
    def _():
        for due, _, move in moves:
            if due >= 24:
                move()
        exchange = [send(part, totals.at[j], sems, (8, j), peer) for j, peer in enumerate(peers)]
        for copy in exchange:
            copy.start()
        total = part[...]
        for copy in exchange:
            copy.wait_recv()
        for j in range(len(peers)):
            total += totals[j]
        out_total[...] = total
        for copy in exchange:
            copy.wait_send()


def summed_gradients(at, b, devices):
    (_, d, t), f = at.shape, b.shape[2]
    low, high = d // devices, f // devices
    vmem = pltpu.VMEM
    whole = pl.BlockSpec(memory_space=vmem)
    operand = lambda i: (2 * (i // 6) + 1 - i // 2 % 3 % 2, 0, 0)
    return pl.pallas_call(
        functools.partial(grads_kernel, devices),
        grid=(12,),
        in_specs=[pl.BlockSpec((pl.squeezed, d, t), operand), pl.BlockSpec((pl.squeezed, t, f // 2), lambda i: (i // 2, 0, i % 2))],
        out_specs=[whole] * 3,
        out_shape=[vmem((4, low, f), BF16), vmem((2, high, d), BF16), vmem((8, 128), F32)],
        scratch_shapes=[
            vmem((2, d, f), BF16), vmem((f, d), BF16), vmem((2, 4, low, f), BF16), vmem((4, high, d), BF16),
            vmem((4, 2, low, f // 2), BF16), vmem((2, 2, high // 2, d), BF16), vmem((4, 2, low, f), BF16), vmem((2, 2, high, d), BF16),
            vmem((8, 128), F32), vmem((devices - 1, 8, 128), F32),
            pltpu.SemaphoreType.DMA((9, 10)), pltpu.SemaphoreType.DMA((9, 10)),
        ],
        compiler_params=pltpu.CompilerParams(vmem_limit_bytes=GRADS_LIMIT, collective_id=0, has_side_effects=True),
        cost_estimate=pl.CostEstimate(flops=12 * t * d * f, bytes_accessed=80 * 2**20, transcendentals=0),
        name="grads",
    )(at, b)


def adamw(w, m, v, g):
    m = 0.9 * m + 0.1 * g
    v = 0.95 * v + 0.05 * g * g
    step = m * lax.rsqrt(v + 1e-8) + 0.1 * w
    return (w - 0.02 * step).astype(BF16), m, v


class Piece:
    def __init__(self, k, place, layer, full, m, v, w_from, m_from, v_from, g, loads, sems):
        self.k, self.place, self.layer, self.full = k, place, layer, full
        self.m, self.v, self.g, self.sems, self.loads = m.at[layer], v.at[layer], g, sems, loads
        self.w_from, self.m_from, self.v_from = w_from, m_from.at[layer], v_from.at[layer]
        self.rows, self.cols = m.shape[1:]
        self.me, self.right, self.left, self.sibling = place.me, place.block(1), place.block(3), place.sibling_block(0)

    def at(self, number, of=None):
        return (self.full if of is None else of).at[self.layer, pl.ds(pl.multiple_of(number * self.rows, 16), self.rows), :]

    def half(self, number, i):
        if self.rows % 32:
            size = self.cols // 2
            return self.full.at[self.layer, pl.ds(pl.multiple_of(number * self.rows, 16), self.rows), pl.ds(i * size, size)]
        size = self.rows // 2
        return self.full.at[self.layer, pl.ds(pl.multiple_of(number * self.rows + i * size, 16), size), :]

    def load(self):
        pairs = ((self.at(self.me, self.w_from), self.at(self.me)), (self.m_from, self.m), (self.v_from, self.v))
        return [pltpu.make_async_copy(src, dst, self.loads.at[self.k, i]) for i, (src, dst) in enumerate(pairs)]

    def update(self, factor):
        w_ref = self.at(self.me)
        for copy in self.load():
            copy.wait()

        def chunk(rows, _):
            w, m, v = adamw(w_ref[rows, :].astype(F32), self.m[rows, :], self.v[rows, :], self.g[rows, :].astype(F32) * factor)
            w_ref[rows, :], self.m[rows, :], self.v[rows, :] = w, m, v

        each_row(self.rows, chunk)

    def copy(self, ref, number, to):
        return send(ref, ref, self.sems, (self.k, number), to)

    def own(self, i):
        return self.copy(self.at(self.me), i, (self.right, self.left, self.sibling)[i])

    def came(self, i):
        return self.copy(self.at((self.left, self.right, self.sibling)[i]), i, self.sibling)

    def on(self, i):
        return self.copy(self.half((self.left, self.right)[i], i), 3 + i, (self.right, self.left)[i])

    def opposite(self, i):
        return self.copy(self.half(self.place.block(2), i), 3 + i, self.sibling)

    def across(self, i):
        return self.copy(self.at((self.left, self.right)[i]) if i < 2 else self.half(self.place.block(2), i - 2), 5 + i, self.sibling)

    def came_across(self, i):
        of = self.place.sibling_block
        return self.copy(self.at(of((3, 1)[i])) if i < 2 else self.half(of(2), i - 2), 5 + i, self.sibling)

    def start(self):
        for i in range(3):
            self.own(i).start()

    def relay(self):
        for i in (0, 1):
            self.came(i).wait_recv()
            self.on(i).start()
            self.across(i).start()

    def finish(self):
        for i in (0, 1):
            self.opposite(i).wait_recv()
            self.across(2 + i).start()

    def end(self):
        self.came(2).wait_recv()
        for i in range(3):
            self.own(i).wait_send()
        for i in (0, 1):
            self.on(i).wait_send()
        for i in range(4):
            self.across(i).wait_send()
            self.came_across(i).wait_recv()


def update_kernel(devices, wide, tall, total, *refs):
    ws, ms, vs, full, new_m, new_v, (loads, sends, recvs) = (refs[i : i + 3] for i in range(0, 21, 3))
    place = Place(devices)
    work = []
    for k in range(6):
        a, layer = (k + 2) % 3, 1 - k // 3
        g = tall.at[1 - layer] if a == 2 else wide.at[2 * (1 - layer) + a]
        work.append(Piece(k, place, layer, full[a], new_m[a], new_v[a], ws[a], ms[a], vs[a], g, loads, (sends, recvs)))
    for piece in work:
        for copy in piece.load():
            copy.start()
    place.barrier([place.block(1), place.block(3), place.sibling_block(0)])
    count = sum(w.shape[0] * w.shape[1] * w.shape[2] for w in ws)
    factor = jnp.minimum(1.0, 0.5 * lax.rsqrt(jnp.sum(total[...], keepdims=True) / count + 1e-30))
    for piece in work:
        piece.update(factor)
        piece.start()
    for k, piece in enumerate(work):
        piece.relay()
        if k:
            work[k - 1].finish()
    work[-1].finish()
    for piece in work:
        piece.end()


def store_kernel(*refs):
    count = len(refs) // 2
    copies = [pltpu.make_async_copy(refs[i], refs[count + i], refs[-1].at[i]) for i in range(count)]
    for copy in copies:
        copy.start()
    for copy in copies:
        copy.wait()


def updated(wide, tall, total, ws, ms, vs, devices):
    out = [*ws, *ms, *vs]
    anywhere, vmem = pl.BlockSpec(memory_space=pl.ANY), pl.BlockSpec(memory_space=pltpu.VMEM)
    new = pl.pallas_call(
        functools.partial(update_kernel, devices),
        in_specs=[vmem] * 3 + [anywhere] * 9,
        out_specs=[vmem] * 9,
        out_shape=[pltpu.VMEM(o.shape, o.dtype) for o in out],
        scratch_shapes=[pltpu.SemaphoreType.DMA((6, 3)), pltpu.SemaphoreType.DMA((6, 9)), pltpu.SemaphoreType.DMA((6, 9))],
        compiler_params=pltpu.CompilerParams(vmem_limit_bytes=4 * 1024 * 1024, collective_id=1, has_side_effects=True),
        name="update",
    )(*[pltpu.with_memory_space_constraint(g, pltpu.VMEM) for g in (wide, tall, total)], *[pltpu.with_memory_space_constraint(o, pltpu.HBM) for o in out])
    return pl.pallas_call(
        store_kernel,
        in_specs=[vmem] * 9,
        out_specs=[anywhere] * 9,
        out_shape=[jax.ShapeDtypeStruct(o.shape, o.dtype) for o in out],
        scratch_shapes=[pltpu.SemaphoreType.DMA((9,))],
        compiler_params=pltpu.CompilerParams(vmem_limit_bytes=1024 * 1024),
        name="store",
    )(*[pltpu.with_memory_space_constraint(n, pltpu.VMEM) for n in new])


def solution(mesh):
    devices = mesh.shape["dp"]

    def body(x, dy, wg, wu, wd, *moments):
        b, at = row_local(x[0], dy[0], wg, wu, wd)
        wide, tall, total = summed_gradients(at, b, devices)
        return tuple(updated(wide, tall, total, (wg, wu, wd), moments[:3], moments[3:], devices))

    data, whole, rows = P(("rep", "dp")), P(), P(None, "dp")
    return jax.shard_map(
        body,
        mesh=mesh,
        in_specs=(data, data, whole, whole, whole, *[rows] * 6),
        out_specs=(*[P("rep")] * 3, *[P("rep", "dp")] * 6),
        check_vma=False,
    )
```

time: 439 us -> 397 us (0.904)
  local copies, waits for them, and re-layouts: 28.7 us -> 0 us
  other arithmetic: 12.8 us -> 0 us
    unnamed x17 -> x0, local copies, waits for them, and re-layouts: 26.7 us -> none
    convert_element_type x2 -> x0, other arithmetic: 11.6 us -> none  [adamw(): return ((w - 0.02 * step).astype(BF16), m, v)]
    pallas_call x3 -> x4, Pallas kernels: 396 us -> 396 us  [the longest x1 140 us: summed_gradients(): pl.pallas_call(functools.partial(grads_kernel, devices), grid=(12,), in_s...]
where the time goes in v2:
time: 397 us
  Pallas kernels  396 us (100%)
    pallas_call x1, Pallas kernels, summed_gradients(): pl.pallas_call(functools.partial(grads_kernel, devices), grid=(12,), in_s...  140 us
    pallas_call x1, Pallas kernels, row_local(): pl.pallas_call(rows_kernel, grid=(t // ROWS,), in_specs=[rows, rows] + [a...  124 us
    pallas_call x1, Pallas kernels, updated(): pl.pallas_call(functools.partial(update_kernel, devices), in_specs=[vmem]...  119 us
    pallas_call x1, Pallas kernels, updated(): pl.pallas_call(store_kernel, in_specs=[vmem] * 9, out_specs=[anywhere] *...  13.5 us

profile of v2, /device:TPU:113, one launch (start us, length us, event | category | flops | bytes accessed | tf_op | source)
XLA Modules:
  0.0 396.7 jit_solution(8069792713979165478)
XLA Ops:
  0.6 123.7 %rows.1 = (bf16[6,2048,2560]{2,1,0:T(8,128)(2,1)}, bf16[4,896,2048]{2,1,0:T(8,128)(2,1)}) custom-call(bf16[2048,896]{1,0:T(8,128)(2,1)} %bitcast.2, bf16[2048,896]{1,0:T(8,128)(2,1)} %bitcast.3, bf16[2,896,2560]{2,1,0:T(8,128)(2,1)} %refs_0_.1, bf16[2,896,2560]{2,1,0:T(8,128)(2,1)} %refs_1_.1, bf16[2,2560,896]{2,1,0:T(8,128)(2,1)} %refs_2_.1), custom_call_target="tpu_custom_call" | custom-call | flops 84557168640 | bytes 157286400 | tf_op jit(solution)/shard_map/rows/pallas_call | solution.py:93
  124.4 139.6 %grads.1 = (bf16[4,112,2560]{2,1,0:T(8,128)(2,1)S(1)}, bf16[2,320,896]{2,1,0:T(8,128)(2,1)S(1)}, f32[8,128]{1,0:T(8,128)S(1)}) custom-call(bf16[4,896,2048]{2,1,0:T(8,128)(2,1)} %get-tuple-element.23.at, bf16[6,2048,2560]{2,1,0:T(8,128)(2,1)} %get-tuple-element.24.b), custom_call_target="tpu_custom_call" | custom-call | flops 56371445760 | bytes 83886080 | tf_op jit(solution)/shard_map/grads/pallas_call | solution.py:298
  264.0 119.1 %update.1 = (bf16[2,896,2560]{2,1,0:T(8,128)(2,1)S(1)}, bf16[2,896,2560]{2,1,0:T(8,128)(2,1)S(1)}, bf16[2,2560,896]{2,1,0:T(8,128)(2,1)S(1)}, f32[2,112,2560]{2,...) custom-call(bf16[4,112,2560]{2,1,0:T(8,128)(2,1)S(1)} %get-tuple-ele, ...), custom_call_target="tpu_custom_call" | custom-call | tf_op jit(solution)/shard_map/update/pallas_call | solution.py:442
  383.1 13.5 %store.1 = (bf16[2,896,2560]{2,1,0:T(8,128)(2,1)}, bf16[2,896,2560]{2,1,0:T(8,128)(2,1)}, bf16[2,2560,896]{2,1,0:T(8,128)(2,1)}, f32[2,112,2560]{2,1,0:T(8,128)}...) custom-call(bf16[2,896,2560]{2,1,0:T(8,128)(2,1)S(1)} %get-tuple-ele, ...), custom_call_target="tpu_custom_call" | custom-call | tf_op jit(solution)/shard_map/store/pallas_call | solution.py:451

commit v3 on v2

--- a/solution.py
+++ b/solution.py
@@ -11,6 +11,7 @@
 VMEM_LIMIT = 63 * 1024 * 1024
 NT = (((1,), (1,)), ((), ()))
 GRADS_LIMIT = 59 * 1024 * 1024
+PART = 512
 ROWS = 256
 
 
@@ -41,6 +42,39 @@
     order = [(wg.at[0], held_wide.at[0]), (wu.at[0], held_wide.at[1]), (wd.at[0], held_down.at[0])]
     order += [(wg.at[1], held_wide.at[2]), (wu.at[1], held_wide.at[3]), (wd.at[1], held_down.at[1])]
     copies = [pltpu.make_async_copy(src, dst, arrived.at[n]) for n, (src, dst) in enumerate(order)]
+    wg0, wu0, wd0, wg1, wu1, wd1 = (dst for _, dst in order)
+    cols = chunks(wg.shape[2], 512)
+
+    def tile(need):
+        a = normed(x[...])
+        at[3] = a.T
+        d = dy[...]
+        at[0] = d.T
+        need(0, 1)
+        for c in cols:
+            gate, up = dot(a, wg0[:, c]), dot(a, wu0[:, c])
+            gate0[:, c], up0[:, c] = gate, up
+            b[4, :, c] = (jax.nn.silu(gate) * up).astype(BF16)
+        need(2)
+        h = x[...] + dot(b[4], wd0[...]).astype(BF16)
+        a = normed(h)
+        at[1] = a.T
+        need(3, 4, 5)
+        for c in cols:
+            gate, up = dot(a, wg1[:, c]), dot(a, wu1[:, c])
+            dact = dot(d, wd1[c, :], NT).astype(BF16).astype(F32)
+            b[2, :, c] = (jax.nn.silu(gate) * up).astype(BF16)
+            b[0, :, c], b[1, :, c] = gated(gate, up, dact)
+        da = (dot(wg1[...], b[0], NT).astype(BF16) + dot(wu1[...], b[1], NT).astype(BF16)).T
+        da, wide = da.astype(F32), h.astype(F32)
+        scale = scale_of(wide)
+        inner = jnp.mean(da * wide, -1, keepdims=True)
+        d = d + (da * scale - wide * (scale * scale * scale * inner)).astype(BF16)
+        at[2] = d.T
+        for c in cols:
+            dact = dot(d, wd0[c, :], NT).astype(BF16).astype(F32)
+            b[3, :, c], b[5, :, c] = gated(gate0[:, c], up0[:, c], dact)
+
     first = pl.program_id(0) == 0
 
     @pl.when(first)
@@ -48,42 +82,15 @@
         for copy in copies:
             copy.start()
 
-    def need(*which):
-        @pl.when(first)
-        def _():
+        def need(*which):
             for n in which:
                 copies[n].wait()
 
-    wg0, wu0, wd0, wg1, wu1, wd1 = (dst for _, dst in order)
-    cols = chunks(wg.shape[2], 512)
-    a = normed(x[...])
-    at[3] = a.T
-    d = dy[...]
-    at[0] = d.T
-    need(0, 1)
-    for c in cols:
-        gate, up = dot(a, wg0[:, c]), dot(a, wu0[:, c])
-        gate0[:, c], up0[:, c] = gate, up
-        b[4, :, c] = (jax.nn.silu(gate) * up).astype(BF16)
-    need(2)
-    h = x[...] + dot(b[4], wd0[...]).astype(BF16)
-    a = normed(h)
-    at[1] = a.T
-    need(3, 4, 5)
-    for c in cols:
-        gate, up = dot(a, wg1[:, c]), dot(a, wu1[:, c])
-        dact = dot(d, wd1[c, :], NT).astype(BF16).astype(F32)
-        b[1, :, c] = (jax.nn.silu(gate) * up).astype(BF16)
-        b[0, :, c], b[2, :, c] = gated(gate, up, dact)
-    da = dot(b[0], wg1[...], NT).astype(BF16) + dot(b[2], wu1[...], NT).astype(BF16)
-    da, wide = da.astype(F32), h.astype(F32)
-    scale = scale_of(wide)
-    inner = jnp.mean(da * wide, -1, keepdims=True)
-    d = d + (da * scale - wide * (scale * scale * scale * inner)).astype(BF16)
-    at[2] = d.T
-    for c in cols:
-        dact = dot(d, wd0[c, :], NT).astype(BF16).astype(F32)
-        b[3, :, c], b[5, :, c] = gated(gate0[:, c], up0[:, c], dact)
+        tile(need)
+
+    @pl.when(jnp.logical_not(first))
+    def _():
+        tile(lambda *which: None)
 
 
 def row_local(x, dy, wg, wu, wd):
@@ -146,7 +153,7 @@
     peers = [(me + j) % devices for j in range(1, devices)]
     sibling = place.sibling_block(0)
     sems = (sends, recvs)
-    low, high = wide.shape[1] // devices, tall.shape[0] // devices
+    low, high = wide.shape[1] // devices, tall.shape[1] // devices
     width = wide.shape[2]
 
     @pl.when(step == 0)
@@ -155,18 +162,18 @@
         place.barrier(peers)
 
     class Sum:
-        def __init__(self, number, k, part):
+        def __init__(self, number, k, ready, start=0, size=None):
             self.number, n = number, k // 3
-            self.is_tall = k % 3 == 1
-            self.ready = 4 * (k + 1) - (2 if part == 0 else 0)
+            self.is_tall, self.ready = k in (2, 4), ready
+            self.end_by = (12, 20, 26, 26, 28, 28 + number % 2)[k]
+            size = size or width
             if self.is_tall:
-                self.rows, self.cols, self.mine, self.sib = high, slice(None), tall, sib_tall
+                self.rows, self.cols, self.mine, self.sib = high, slice(None), tall.at[n], sib_tall.at[n]
                 self.transit, self.end, self.out = [transit_tall.at[n, i] for i in (0, 1)], [end_tall.at[n, i] for i in (0, 1)], out_tall.at[n]
                 self.halves = [(pl.ds(i * high // 2, high // 2), slice(None)) for i in (0, 1)]
             else:
-                slot = k % 3 // 2
+                slot = (k % 3 + 1) // 2
                 at = 2 * n + slot
-                start, size = (0, width) if part is None else (part * width // 2, width // 2)
                 self.rows, self.cols, self.mine, self.sib = low, pl.ds(start, size), wide.at[slot], sib_wide.at[slot]
                 c = size // 2
                 self.transit = [transit_wide.at[at, i, :, pl.ds(start // 2, c)] for i in (0, 1)]
@@ -243,11 +250,13 @@
                 for j in (0, 1):
                     self.to_end(i, j).wait_send()
 
-    sums = [Sum(n, *of) for n, of in enumerate(((0, 0), (0, 1), (1, None), (2, None), (3, None), (4, None), (5, 0), (5, 1)))]
+    half = width // 2
+    parts = [(0, 1, 0, PART), (0, 2, PART, half - PART), (0, 4, half, half), (1, 6, 0, half), (1, 8, half, half)]
+    parts += [(2, 12), (3, 16), (4, 20), (5, 22, 0, half), (5, 24, half, half)]
+    sums = [Sum(n, *of) for n, of in enumerate(parts)]
     moves = []
     for n, one in enumerate(sums):
-        after = sums[n + 1].ready + 3 if n + 1 < len(sums) else one.ready + 4
-        moves += [(one.ready, 0, one.start), (one.ready + 1, 1, one.first), (one.ready + 3, 2, one.second), (after, 3, one.last)]
+        moves += [(one.ready, 0, one.start), (one.ready + 1, 1, one.first), (one.ready + (2 if n == 1 else 3), 2, one.second), (one.end_by, 3, one.last)]
     moves.sort(key=lambda move: move[:2])
 
     def at_point(point):
@@ -258,25 +267,27 @@
     def compute(start, size):
         cols = pl.ds(start, size)
 
-        @pl.when(which % 3 == 1)
+        is_tall = (which % 2 == 0) & (which > 0)
+
+        @pl.when(is_tall)
         def _():
-            tall[pl.ds(pl.multiple_of(side * (width // 2) + start, 256), size), :] = dot(at[...], b[:, cols]).astype(BF16).T
-
-        @pl.when(which % 3 != 1)
+            tall[which // 2 - 1, pl.ds(pl.multiple_of(side * half + start, 256), size), :] = dot(at[...], b[:, cols]).astype(BF16).T
+
+        @pl.when(jnp.logical_not(is_tall))
         def _():
-            wide[which % 3 // 2, :, pl.ds(pl.multiple_of(side * (width // 2) + start, 256), size)] = dot(at[...], b[:, cols]).astype(BF16)
+            wide[(which % 3 + 1) // 2, :, pl.ds(pl.multiple_of(side * half + start, 256), size)] = dot(at[...], b[:, cols]).astype(BF16)
 
     at_point(0)
-    compute(0, 512)
+    compute(0, PART)
     at_point(1)
-    compute(512, width // 2 - 512)
+    compute(PART, half - PART)
 
     @pl.when(step == 11)
     def _():
         for due, _, move in moves:
             if due >= 24:
                 move()
-        exchange = [send(part, totals.at[j], sems, (8, j), peer) for j, peer in enumerate(peers)]
+        exchange = [send(part, totals.at[j], sems, (len(sums), j), peer) for j, peer in enumerate(peers)]
         for copy in exchange:
             copy.start()
         total = part[...]
@@ -294,7 +305,7 @@
     low, high = d // devices, f // devices
     vmem = pltpu.VMEM
     whole = pl.BlockSpec(memory_space=vmem)
-    operand = lambda i: (2 * (i // 6) + 1 - i // 2 % 3 % 2, 0, 0)
+    operand = lambda i: (2 * (i // 6) + 1 - (1 - i // 2 % 2) * ((i // 2 + 5) // 6), 0, 0)
     return pl.pallas_call(
         functools.partial(grads_kernel, devices),
         grid=(12,),
@@ -302,10 +313,10 @@
         out_specs=[whole] * 3,
         out_shape=[vmem((4, low, f), BF16), vmem((2, high, d), BF16), vmem((8, 128), F32)],
         scratch_shapes=[
-            vmem((2, d, f), BF16), vmem((f, d), BF16), vmem((2, 4, low, f), BF16), vmem((4, high, d), BF16),
+            vmem((2, d, f), BF16), vmem((2, f, d), BF16), vmem((2, 4, low, f), BF16), vmem((2, 4, high, d), BF16),
             vmem((4, 2, low, f // 2), BF16), vmem((2, 2, high // 2, d), BF16), vmem((4, 2, low, f), BF16), vmem((2, 2, high, d), BF16),
             vmem((8, 128), F32), vmem((devices - 1, 8, 128), F32),
-            pltpu.SemaphoreType.DMA((9, 10)), pltpu.SemaphoreType.DMA((9, 10)),
+            pltpu.SemaphoreType.DMA((11, 10)), pltpu.SemaphoreType.DMA((11, 10)),
         ],
         compiler_params=pltpu.CompilerParams(vmem_limit_bytes=GRADS_LIMIT, collective_id=0, has_side_effects=True),
         cost_estimate=pl.CostEstimate(flops=12 * t * d * f, bytes_accessed=80 * 2**20, transcendentals=0),
@@ -409,15 +420,17 @@
         a, layer = (k + 2) % 3, 1 - k // 3
         g = tall.at[1 - layer] if a == 2 else wide.at[2 * (1 - layer) + a]
         work.append(Piece(k, place, layer, full[a], new_m[a], new_v[a], ws[a], ms[a], vs[a], g, loads, (sends, recvs)))
-    for piece in work:
+    for piece in work[:2]:
         for copy in piece.load():
             copy.start()
     place.barrier([place.block(1), place.block(3), place.sibling_block(0)])
     count = sum(w.shape[0] * w.shape[1] * w.shape[2] for w in ws)
     factor = jnp.minimum(1.0, 0.5 * lax.rsqrt(jnp.sum(total[...], keepdims=True) / count + 1e-30))
-    for piece in work:
+    for k, piece in enumerate(work):
         piece.update(factor)
         piece.start()
+        for copy in work[k + 2].load() if k + 2 < len(work) else []:
+            copy.start()
     for k, piece in enumerate(work):
         piece.relay()
         if k:

time: 397 us -> 384 us (0.967)
  Pallas kernels: 396 us -> 383 us
    pallas_call x1, Pallas kernels: 140 us -> 132 us  [summed_gradients(): pl.pallas_call(functools.partial(grads_kernel, devices), grid=(12,), in_s...]
    pallas_call x1, Pallas kernels: 124 us -> 118 us  [row_local(): pl.pallas_call(rows_kernel, grid=(t // ROWS,), in_specs=[rows, rows] + [a...]
where the time goes in v3:
time: 384 us
  Pallas kernels  383 us (100%)
    pallas_call x1, Pallas kernels, summed_gradients(): pl.pallas_call(functools.partial(grads_kernel, devices), grid=(12,), in_s...  132 us
    pallas_call x1, Pallas kernels, updated(): pl.pallas_call(functools.partial(update_kernel, devices), in_specs=[vmem]...  119 us
    pallas_call x1, Pallas kernels, row_local(): pl.pallas_call(rows_kernel, grid=(t // ROWS,), in_specs=[rows, rows] + [a...  118 us
    pallas_call x1, Pallas kernels, updated(): pl.pallas_call(store_kernel, in_specs=[vmem] * 9, out_specs=[anywhere] *...  13.5 us

profile of v3, /device:TPU:113, one launch (start us, length us, event | category | flops | bytes accessed | tf_op | source)
XLA Modules:
  0.0 383.6 jit_solution(11574714783600958438)
XLA Ops:
  0.6 118.2 %rows.1 = (bf16[6,2048,2560]{2,1,0:T(8,128)(2,1)}, bf16[4,896,2048]{2,1,0:T(8,128)(2,1)}) custom-call(bf16[2048,896]{1,0:T(8,128)(2,1)} %bitcast.2, bf16[2048,896]{1,0:T(8,128)(2,1)} %bitcast.3, bf16[2,896,2560]{2,1,0:T(8,128)(2,1)} %refs_0_.1, bf16[2,896,2560]{2,1,0:T(8,128)(2,1)} %refs_1_.1, bf16[2,2560,896]{2,1,0:T(8,128)(2,1)} %refs_2_.1), custom_call_target="tpu_custom_call" | custom-call | flops 84557168640 | bytes 157286400 | tf_op jit(solution)/shard_map/rows/pallas_call | solution.py:100
  118.9 132.4 %grads.1 = (bf16[4,112,2560]{2,1,0:T(8,128)(2,1)S(1)}, bf16[2,320,896]{2,1,0:T(8,128)(2,1)S(1)}, f32[8,128]{1,0:T(8,128)S(1)}) custom-call(bf16[4,896,2048]{2,1,0:T(8,128)(2,1)} %get-tuple-element.23.at, bf16[6,2048,2560]{2,1,0:T(8,128)(2,1)} %get-tuple-element.24.b), custom_call_target="tpu_custom_call" | custom-call | flops 56371445760 | bytes 83886080 | tf_op jit(solution)/shard_map/grads/pallas_call | solution.py:309
  251.3 118.8 %update.1 = (bf16[2,896,2560]{2,1,0:T(8,128)(2,1)S(1)}, bf16[2,896,2560]{2,1,0:T(8,128)(2,1)S(1)}, bf16[2,2560,896]{2,1,0:T(8,128)(2,1)S(1)}, f32[2,112,2560]{2,...) custom-call(bf16[4,112,2560]{2,1,0:T(8,128)(2,1)S(1)} %get-tuple-ele, ...), custom_call_target="tpu_custom_call" | custom-call | tf_op jit(solution)/shard_map/update/pallas_call | solution.py:455
  370.0 13.5 %store.1 = (bf16[2,896,2560]{2,1,0:T(8,128)(2,1)}, bf16[2,896,2560]{2,1,0:T(8,128)(2,1)}, bf16[2,2560,896]{2,1,0:T(8,128)(2,1)}, f32[2,112,2560]{2,1,0:T(8,128)}...) custom-call(bf16[2,896,2560]{2,1,0:T(8,128)(2,1)S(1)} %get-tuple-ele, ...), custom_call_target="tpu_custom_call" | custom-call | tf_op jit(solution)/shard_map/store/pallas_call | solution.py:464

commit v4 on v3

--- a/solution.py
+++ b/solution.py
@@ -10,8 +10,8 @@
 F32, BF16 = jnp.float32, jnp.bfloat16
 VMEM_LIMIT = 63 * 1024 * 1024
 NT = (((1,), (1,)), ((), ()))
-GRADS_LIMIT = 59 * 1024 * 1024
-PART = 512
+GRADS_LIMIT = 61850 * 1024
+TILE, FEW = 512, 256
 ROWS = 256
 
 
@@ -38,7 +38,7 @@
     return (dact * up * (s + silu * (1 - s))).astype(BF16), (dact * silu).astype(BF16)
 
 
-def rows_kernel(x, dy, wg, wu, wd, b, at, gate0, up0, held_wide, held_down, arrived):
+def rows_kernel(x, dy, wg, wu, wd, b, gu, at, dh, held_wide, held_down, arrived):
     order = [(wg.at[0], held_wide.at[0]), (wu.at[0], held_wide.at[1]), (wd.at[0], held_down.at[0])]
     order += [(wg.at[1], held_wide.at[2]), (wu.at[1], held_wide.at[3]), (wd.at[1], held_down.at[1])]
     copies = [pltpu.make_async_copy(src, dst, arrived.at[n]) for n, (src, dst) in enumerate(order)]
@@ -53,10 +53,10 @@
         need(0, 1)
         for c in cols:
             gate, up = dot(a, wg0[:, c]), dot(a, wu0[:, c])
-            gate0[:, c], up0[:, c] = gate, up
-            b[4, :, c] = (jax.nn.silu(gate) * up).astype(BF16)
+            gu[0, :, c], gu[1, :, c] = gate, up
+            b[3, :, c] = (jax.nn.silu(gate) * up).astype(BF16)
         need(2)
-        h = x[...] + dot(b[4], wd0[...]).astype(BF16)
+        h = x[...] + dot(b[3], wd0[...]).astype(BF16)
         a = normed(h)
         at[1] = a.T
         need(3, 4, 5)
@@ -70,10 +70,8 @@
         scale = scale_of(wide)
         inner = jnp.mean(da * wide, -1, keepdims=True)
         d = d + (da * scale - wide * (scale * scale * scale * inner)).astype(BF16)
+        dh[...] = d
         at[2] = d.T
-        for c in cols:
-            dact = dot(d, wd0[c, :], NT).astype(BF16).astype(F32)
-            b[3, :, c], b[5, :, c] = gated(gate0[:, c], up0[:, c], dact)
 
     first = pl.program_id(0) == 0
 
@@ -101,14 +99,20 @@
         rows_kernel,
         grid=(t // ROWS,),
         in_specs=[rows, rows] + [anywhere] * 3,
-        out_specs=[pl.BlockSpec((6, ROWS, f), lambda i: (0, i, 0)), pl.BlockSpec((4, d, ROWS), lambda i: (0, 0, i))],
-        out_shape=[jax.ShapeDtypeStruct((6, t, f), BF16), jax.ShapeDtypeStruct((4, d, t), BF16)],
+        out_specs=[
+            pl.BlockSpec((4, ROWS, f), lambda i: (0, i, 0)), pl.BlockSpec((2, ROWS, f), lambda i: (0, i, 0)),
+            pl.BlockSpec((4, d, ROWS), lambda i: (0, 0, i)), rows,
+        ],
+        out_shape=[
+            jax.ShapeDtypeStruct((4, t, f), BF16), jax.ShapeDtypeStruct((2, t, f), F32), jax.ShapeDtypeStruct((4, d, t), BF16),
+            jax.ShapeDtypeStruct((t, d), BF16),
+        ],
         scratch_shapes=[
-            pltpu.VMEM((ROWS, f), F32), pltpu.VMEM((ROWS, f), F32), pltpu.VMEM((4, d, f), BF16), pltpu.VMEM((2, f, d), BF16),
+            pltpu.VMEM((4, d, f), BF16), pltpu.VMEM((2, f, d), BF16),
             pltpu.SemaphoreType.DMA((6,)),
         ],
         compiler_params=pltpu.CompilerParams(vmem_limit_bytes=VMEM_LIMIT),
-        cost_estimate=pl.CostEstimate(flops=18 * t * d * f, bytes_accessed=150 * 2**20, transcendentals=0),
+        cost_estimate=pl.CostEstimate(flops=16 * t * d * f, bytes_accessed=150 * 2**20, transcendentals=0),
         name="rows",
     )(x, dy, wg, wu, wd)
 
@@ -144,10 +148,11 @@
 
 
 def grads_kernel(
-    devices, at, b, out_wide, out_tall, out_total, wide, tall, sib_wide, sib_tall, transit_wide, transit_tall, end_wide, end_tall, part, totals, sends, recvs
+    devices, at, b, wd, gu_from, dh_from, out_wide, out_tall, out_total,
+    wide, tall, sib_wide, sib_tall, transit_wide, transit_tall, end_wide, end_tall, gu, dh, both, part, totals, loaded, sends, recvs,
 ):
     step = pl.program_id(0)
-    which, side = step // 2, step % 2
+    which, tile = step // 5, step % 5
     place = Place(devices)
     me = place.me
     peers = [(me + j) % devices for j in range(1, devices)]
@@ -164,20 +169,20 @@
     class Sum:
         def __init__(self, number, k, ready, start=0, size=None):
             self.number, n = number, k // 3
-            self.is_tall, self.ready = k in (2, 4), ready
-            self.end_by = (12, 20, 26, 26, 28, 28 + number % 2)[k]
+            self.is_tall, self.ready = k in (2, 3), ready
+            self.end_by = (20, 20, 32, 32, 33, 33)[k]
             size = size or width
             if self.is_tall:
                 self.rows, self.cols, self.mine, self.sib = high, slice(None), tall.at[n], sib_tall.at[n]
                 self.transit, self.end, self.out = [transit_tall.at[n, i] for i in (0, 1)], [end_tall.at[n, i] for i in (0, 1)], out_tall.at[n]
                 self.halves = [(pl.ds(i * high // 2, high // 2), slice(None)) for i in (0, 1)]
             else:
-                slot = (k % 3 + 1) // 2
+                slot = k % 4
                 at = 2 * n + slot
                 self.rows, self.cols, self.mine, self.sib = low, pl.ds(start, size), wide.at[slot], sib_wide.at[slot]
                 c = size // 2
-                self.transit = [transit_wide.at[at, i, :, pl.ds(start // 2, c)] for i in (0, 1)]
-                self.end, self.out = [end_wide.at[at, i] for i in (0, 1)], out_wide.at[at]
+                self.transit = [transit_wide.at[slot, i, :, pl.ds(start // 2, c)] for i in (0, 1)]
+                self.end, self.out = [end_wide.at[slot, i] for i in (0, 1)], out_wide.at[at]
                 self.halves = [(slice(None), pl.ds(start + i * c, c)) for i in (0, 1)]
 
         def block(self, number):
@@ -250,42 +255,66 @@
                 for j in (0, 1):
                     self.to_end(i, j).wait_send()
 
-    half = width // 2
-    parts = [(0, 1, 0, PART), (0, 2, PART, half - PART), (0, 4, half, half), (1, 6, 0, half), (1, 8, half, half)]
-    parts += [(2, 12), (3, 16), (4, 20), (5, 22, 0, half), (5, 24, half, half)]
+    parts = [(0, 1, 0, TILE), (0, 3, TILE, 2 * TILE), (0, 5, 3 * TILE, 2 * TILE), (1, 7, 0, 2 * TILE), (1, 10, 2 * TILE, 3 * TILE)]
+    parts += [(2, 15), (3, 20)] + [(k, ready, at * FEW, size * FEW) for ready, at, size in ((24, 0, 4), (27, 4, 3), (30, 7, 3)) for k in (4, 5)]
     sums = [Sum(n, *of) for n, of in enumerate(parts)]
     moves = []
-    for n, one in enumerate(sums):
-        moves += [(one.ready, 0, one.start), (one.ready + 1, 1, one.first), (one.ready + (2 if n == 1 else 3), 2, one.second), (one.end_by, 3, one.last)]
+    for one in sums:
+        moves += [(one.ready, 0, one.start), (one.ready + 1, 1, one.first), (one.ready + 3 - one.ready // 30, 2, one.second), (one.end_by, 3, one.last)]
     moves.sort(key=lambda move: move[:2])
-
-    def at_point(point):
+    for due in range(30):
+        now = [move for when, _, move in moves if when == due]
+        if now:
+
+            @pl.when(step == due)
+            def _():
+                for move in now:
+                    move()
+
+    def columns(number):
+        cols = pl.ds(pl.multiple_of(number * FEW, FEW), FEW)
+        return pltpu.make_async_copy(gu_from.at[:, :, cols], gu.at[number % 2], loaded.at[number % 2])
+
+    rest = pltpu.make_async_copy(dh_from, dh, loaded.at[2])
+    column = step - 20
+
+    @pl.when(step == 1)
+    def _():
+        rest.start()
+
+    @pl.when((step >= 19) & (step < 29))
+    def _():
+        columns(column + 1).start()
+
+    @pl.when(step < 20)
+    def _():
+        @pl.when(which >= 2)
+        def _():
+            tall[which - 2, pl.ds(pl.multiple_of(tile * TILE, TILE), TILE), :] = dot(at[...], b[...]).astype(BF16).T
+
+        @pl.when(which < 2)
+        def _():
+            wide[which, :, pl.ds(pl.multiple_of(tile * TILE, TILE), TILE)] = dot(at[...], b[...]).astype(BF16)
+
+    @pl.when(step == 20)
+    def _():
+        rest.wait()
+
+    @pl.when(step >= 20)
+    def _():
+        columns(column).wait()
+        held = gu.at[column % 2]
+        for r in chunks(dh.shape[0], 512):
+            dact = dot(dh[r, :], wd[...], NT).astype(BF16).astype(F32)
+            both[r, :FEW], both[r, FEW:] = gated(held[0, r, :], held[1, r, :], dact)
+        cols = pl.ds(pl.multiple_of(column * FEW, FEW), FEW)
+        g = dot(at[...], both[...]).astype(BF16)
+        wide[0, :, cols], wide[1, :, cols] = g[:, :FEW], g[:, FEW:]
+
+    @pl.when(step == 29)
+    def _():
         for due, _, move in moves:
-            if due % 2 == point and due < 24:
-                pl.when(step == due // 2)(move)
-
-    def compute(start, size):
-        cols = pl.ds(start, size)
-
-        is_tall = (which % 2 == 0) & (which > 0)
-
-        @pl.when(is_tall)
-        def _():
-            tall[which // 2 - 1, pl.ds(pl.multiple_of(side * half + start, 256), size), :] = dot(at[...], b[:, cols]).astype(BF16).T
-
-        @pl.when(jnp.logical_not(is_tall))
-        def _():
-            wide[(which % 3 + 1) // 2, :, pl.ds(pl.multiple_of(side * half + start, 256), size)] = dot(at[...], b[:, cols]).astype(BF16)
-
-    at_point(0)
-    compute(0, PART)
-    at_point(1)
-    compute(PART, half - PART)
-
-    @pl.when(step == 11)
-    def _():
-        for due, _, move in moves:
-            if due >= 24:
+            if due >= 30:
                 move()
         exchange = [send(part, totals.at[j], sems, (len(sums), j), peer) for j, peer in enumerate(peers)]
         for copy in exchange:
@@ -300,28 +329,33 @@
             copy.wait_send()
 
 
-def summed_gradients(at, b, devices):
+def summed_gradients(at, b, wd, gu, dh, devices):
     (_, d, t), f = at.shape, b.shape[2]
     low, high = d // devices, f // devices
     vmem = pltpu.VMEM
-    whole = pl.BlockSpec(memory_space=vmem)
-    operand = lambda i: (2 * (i // 6) + 1 - (1 - i // 2 % 2) * ((i // 2 + 5) // 6), 0, 0)
+    whole, anywhere = pl.BlockSpec(memory_space=vmem), pl.BlockSpec(memory_space=pl.ANY)
+    operand = lambda i: (1 - i // 10 + 2 * (i // 15) + 2 * (i // 20), 0, 0)
+    tile = lambda i: (jnp.minimum(i, 19) // 5, 0, jnp.minimum(i, 19) % 5)
     return pl.pallas_call(
         functools.partial(grads_kernel, devices),
-        grid=(12,),
-        in_specs=[pl.BlockSpec((pl.squeezed, d, t), operand), pl.BlockSpec((pl.squeezed, t, f // 2), lambda i: (i // 2, 0, i % 2))],
+        grid=(30,),
+        in_specs=[
+            pl.BlockSpec((pl.squeezed, d, t), operand), pl.BlockSpec((pl.squeezed, t, TILE), tile),
+            pl.BlockSpec((pl.squeezed, FEW, d), lambda i: (0, jnp.maximum(i - 20, 0), 0)), anywhere, anywhere,
+        ],
         out_specs=[whole] * 3,
         out_shape=[vmem((4, low, f), BF16), vmem((2, high, d), BF16), vmem((8, 128), F32)],
         scratch_shapes=[
             vmem((2, d, f), BF16), vmem((2, f, d), BF16), vmem((2, 4, low, f), BF16), vmem((2, 4, high, d), BF16),
-            vmem((4, 2, low, f // 2), BF16), vmem((2, 2, high // 2, d), BF16), vmem((4, 2, low, f), BF16), vmem((2, 2, high, d), BF16),
+            vmem((2, 2, low, f // 2), BF16), vmem((2, 2, high // 2, d), BF16), vmem((2, 2, low, f), BF16), vmem((2, 2, high, d), BF16),
+            vmem((2, 2, t, FEW), F32), vmem((t, d), BF16), vmem((t, 2 * FEW), BF16),
             vmem((8, 128), F32), vmem((devices - 1, 8, 128), F32),
-            pltpu.SemaphoreType.DMA((11, 10)), pltpu.SemaphoreType.DMA((11, 10)),
+            pltpu.SemaphoreType.DMA((3,)), pltpu.SemaphoreType.DMA((14, 10)), pltpu.SemaphoreType.DMA((14, 10)),
         ],
         compiler_params=pltpu.CompilerParams(vmem_limit_bytes=GRADS_LIMIT, collective_id=0, has_side_effects=True),
-        cost_estimate=pl.CostEstimate(flops=12 * t * d * f, bytes_accessed=80 * 2**20, transcendentals=0),
+        cost_estimate=pl.CostEstimate(flops=14 * t * d * f, bytes_accessed=120 * 2**20, transcendentals=0),
         name="grads",
-    )(at, b)
+    )(at, b, wd, *[pltpu.with_memory_space_constraint(one, pltpu.HBM) for one in (gu, dh)])
 
 
 def adamw(w, m, v, g):
@@ -476,8 +510,8 @@
     devices = mesh.shape["dp"]
 
     def body(x, dy, wg, wu, wd, *moments):
-        b, at = row_local(x[0], dy[0], wg, wu, wd)
-        wide, tall, total = summed_gradients(at, b, devices)
+        b, gu, at, dh = row_local(x[0], dy[0], wg, wu, wd)
+        wide, tall, total = summed_gradients(at, b, wd, gu, dh, devices)
         return tuple(updated(wide, tall, total, (wg, wu, wd), moments[:3], moments[3:], devices))
 
     data, whole, rows = P(("rep", "dp")), P(), P(None, "dp")

time: 384 us -> 375 us (0.977)
  Pallas kernels: 383 us -> 374 us
    pallas_call x1, Pallas kernels: 118 us -> 105 us  [row_local(): pl.pallas_call(rows_kernel, grid=(t // ROWS,), in_specs=[rows, rows] + [a...]
    pallas_call x1, Pallas kernels: 132 us -> 137 us  [summed_gradients(): pl.pallas_call(functools.partial(grads_kernel, devices), grid=(30,), in_s...]
where the time goes in v4:
time: 375 us
  Pallas kernels  374 us (100%)
    pallas_call x1, Pallas kernels, summed_gradients(): pl.pallas_call(functools.partial(grads_kernel, devices), grid=(30,), in_s...  137 us
    pallas_call x1, Pallas kernels, updated(): pl.pallas_call(functools.partial(update_kernel, devices), in_specs=[vmem]...  119 us
    pallas_call x1, Pallas kernels, row_local(): pl.pallas_call(rows_kernel, grid=(t // ROWS,), in_specs=[rows, rows] + [a...  105 us
    pallas_call x1, Pallas kernels, updated(): pl.pallas_call(store_kernel, in_specs=[vmem] * 9, out_specs=[anywhere] *...  13.5 us

profile of v4, /device:TPU:113, one launch (start us, length us, event | category | flops | bytes accessed | tf_op | source)
XLA Modules:
  0.0 375.0 jit_solution(9418538008780047960)
XLA Ops:
  0.6 104.8 %rows.1 = (bf16[4,2048,2560]{2,1,0:T(8,128)(2,1)}, f32[2,2048,2560]{2,1,0:T(8,128)}, bf16[4,896,2048]{2,1,0:T(8,128)(2,1)}, bf16[2048,896]{1,0:T(8,128)(2,1)}) custom-call(bf16[2048,896]{1,0:T(8,128)(2,1)} %bitcast.2, bf16[2048,896]{1,0:T(8,128)(2,1)} %bitcast.3, bf16[2,896,2560]{2,1,0:T(8,128)(2,1)} %refs_0_.1, bf16[2,896,2560]{2,1,0:T(8,128)(2,1)} %refs_1_.1, ...), custom_call_target="tpu_custom_call" | custom-call | flops 75161927680 | bytes 157286400 | tf_op jit(solution)/shard_map/rows/pallas_call | solution.py:98
  105.4 137.2 %grads.1 = (bf16[4,112,2560]{2,1,0:T(8,128)(2,1)S(1)}, bf16[2,320,896]{2,1,0:T(8,128)(2,1)S(1)}, f32[8,128]{1,0:T(8,128)S(1)}) custom-call(bf16[4,896,2048]{2,1,0:T(8,128)(2,1)} %get-tuple-element.25.at, bf16[4,2048,2560]{2,1,0:T(8,128)(2,1)} %get-tuple-element.26.b, bf16[2,2560,896]{2,1,0:T(8,128)(2,1)} %refs_2_.1, ...), custom_call_target="tpu_custom_call" | custom-call | flops 65766686720 | bytes 125829120 | tf_op jit(solution)/shard_map/grads/pallas_call | solution.py:339
  242.6 118.8 %update.1 = (bf16[2,896,2560]{2,1,0:T(8,128)(2,1)S(1)}, bf16[2,896,2560]{2,1,0:T(8,128)(2,1)S(1)}, bf16[2,2560,896]{2,1,0:T(8,128)(2,1)S(1)}, f32[2,112,2560]{2,...) custom-call(bf16[4,112,2560]{2,1,0:T(8,128)(2,1)S(1)} %get-tuple-ele, ...), custom_call_target="tpu_custom_call" | custom-call | tf_op jit(solution)/shard_map/update/pallas_call | solution.py:489
  361.4 13.5 %store.1 = (bf16[2,896,2560]{2,1,0:T(8,128)(2,1)}, bf16[2,896,2560]{2,1,0:T(8,128)(2,1)}, bf16[2,2560,896]{2,1,0:T(8,128)(2,1)}, f32[2,112,2560]{2,1,0:T(8,128)}...) custom-call(bf16[2,896,2560]{2,1,0:T(8,128)(2,1)S(1)} %get-tuple-ele, ...), custom_call_target="tpu_custom_call" | custom-call | tf_op jit(solution)/shard_map/store/pallas_call | solution.py:498

commit v5 on v4

--- a/solution.py
+++ b/solution.py
@@ -170,6 +170,7 @@
         def __init__(self, number, k, ready, start=0, size=None):
             self.number, n = number, k // 3
             self.is_tall, self.ready = k in (2, 3), ready
+            self.patience = 2 if ready == 30 else 4 if 1 < ready < 20 else 3
             self.end_by = (20, 20, 32, 32, 33, 33)[k]
             size = size or width
             if self.is_tall:
@@ -260,7 +261,7 @@
     sums = [Sum(n, *of) for n, of in enumerate(parts)]
     moves = []
     for one in sums:
-        moves += [(one.ready, 0, one.start), (one.ready + 1, 1, one.first), (one.ready + 3 - one.ready // 30, 2, one.second), (one.end_by, 3, one.last)]
+        moves += [(one.ready, 0, one.start), (one.ready + 1, 1, one.first), (one.ready + one.patience, 2, one.second), (one.end_by, 3, one.last)]
     moves.sort(key=lambda move: move[:2])
     for due in range(30):
         now = [move for when, _, move in moves if when == due]

time: 375 us -> 372 us (level)
  no operation moved by 1% of the time
where the time goes in v5:
time: 372 us
  Pallas kernels  371 us (100%)
    pallas_call x1, Pallas kernels, summed_gradients(): pl.pallas_call(functools.partial(grads_kernel, devices), grid=(30,), in_s...  134 us
    pallas_call x1, Pallas kernels, updated(): pl.pallas_call(functools.partial(update_kernel, devices), in_specs=[vmem]...  119 us
    pallas_call x1, Pallas kernels, row_local(): pl.pallas_call(rows_kernel, grid=(t // ROWS,), in_specs=[rows, rows] + [a...  105 us
    pallas_call x1, Pallas kernels, updated(): pl.pallas_call(store_kernel, in_specs=[vmem] * 9, out_specs=[anywhere] *...  13.5 us

profile of v5, /device:TPU:113, one launch (start us, length us, event | category | flops | bytes accessed | tf_op | source)
XLA Modules:
  0.0 371.8 jit_solution(7149679600608441839)
XLA Ops:
  0.6 104.8 %rows.1 = (bf16[4,2048,2560]{2,1,0:T(8,128)(2,1)}, f32[2,2048,2560]{2,1,0:T(8,128)}, bf16[4,896,2048]{2,1,0:T(8,128)(2,1)}, bf16[2048,896]{1,0:T(8,128)(2,1)}) custom-call(bf16[2048,896]{1,0:T(8,128)(2,1)} %bitcast.2, bf16[2048,896]{1,0:T(8,128)(2,1)} %bitcast.3, bf16[2,896,2560]{2,1,0:T(8,128)(2,1)} %refs_0_.1, bf16[2,896,2560]{2,1,0:T(8,128)(2,1)} %refs_1_.1, ...), custom_call_target="tpu_custom_call" | custom-call | flops 75161927680 | bytes 157286400 | tf_op jit(solution)/shard_map/rows/pallas_call | solution.py:98
  105.4 133.9 %grads.1 = (bf16[4,112,2560]{2,1,0:T(8,128)(2,1)S(1)}, bf16[2,320,896]{2,1,0:T(8,128)(2,1)S(1)}, f32[8,128]{1,0:T(8,128)S(1)}) custom-call(bf16[4,896,2048]{2,1,0:T(8,128)(2,1)} %get-tuple-element.25.at, bf16[4,2048,2560]{2,1,0:T(8,128)(2,1)} %get-tuple-element.26.b, bf16[2,2560,896]{2,1,0:T(8,128)(2,1)} %refs_2_.1, ...), custom_call_target="tpu_custom_call" | custom-call | flops 65766686720 | bytes 125829120 | tf_op jit(solution)/shard_map/grads/pallas_call | solution.py:340
  239.3 118.8 %update.1 = (bf16[2,896,2560]{2,1,0:T(8,128)(2,1)S(1)}, bf16[2,896,2560]{2,1,0:T(8,128)(2,1)S(1)}, bf16[2,2560,896]{2,1,0:T(8,128)(2,1)S(1)}, f32[2,112,2560]{2,...) custom-call(bf16[4,112,2560]{2,1,0:T(8,128)(2,1)S(1)} %get-tuple-ele, ...), custom_call_target="tpu_custom_call" | custom-call | tf_op jit(solution)/shard_map/update/pallas_call | solution.py:490
  358.1 13.5 %store.1 = (bf16[2,896,2560]{2,1,0:T(8,128)(2,1)}, bf16[2,896,2560]{2,1,0:T(8,128)(2,1)}, bf16[2,2560,896]{2,1,0:T(8,128)(2,1)}, f32[2,112,2560]{2,1,0:T(8,128)}...) custom-call(bf16[2,896,2560]{2,1,0:T(8,128)(2,1)S(1)} %get-tuple-ele, ...), custom_call_target="tpu_custom_call" | custom-call | tf_op jit(solution)/shard_map/store/pallas_call | solution.py:499
